TPU v7x, 256 devices: a whole 4x4x8 slice. The times are simulated.
256 devices in a mesh: section: 8 (over z), dp: 32 (over x, y, core).
Axes of the slice: x: 4, y: 4, z: 8, core: 2. Of those that a mesh axis runs over, the one named last changes fastest.
Arguments:
- entry: bfloat16 [6144, 3584], P('dp'), may hold values from -6 to 6
- norm_gain: float32 [8, 3584], P('section'), may hold values from 0.5 to 1.5
- w_qkv: bfloat16 [8, 3584, 1152], P('section', 'dp'), may hold values from -0.09375 to 0.09375
- w_out: bfloat16 [8, 896, 3584], P('section', 'dp'), may hold values from -0.1875 to 0.1875
- final_gain: float32 [3584], replicated, may hold values from 0.5 to 1.5
- lengths: int32 [128], P('dp'), may hold values from 24 to 48
- positive: int32 [64], P('dp'), may hold values from 0 to 63, each once
Outputs:
- section_grads: bfloat16 [8, 6144, 3584], P('section', 'dp')
Inputs may be any that keep to these rules, and one draw needn't show every extreme that they name: lengths[j] is the count of tokens of sequence j; its last token is pooled. Each document index is the positive of exactly one query.
All inputs are finite; a program needn't handle non-finite values.
Results may differ from a plain program's by a relative error of at most 0.022.
Values may be sent and summed in bfloat16 or wider, within the bound.
No kernel may reach another device: no remote copies, remote signals or barrier semaphores. Data moves between devices by JAX's collectives and lax.ppermute only.
A program may use at most 192 MiB of HBM per device.

v0:
```python
import jax
import jax.numpy as jnp
from jax import lax
from jax.sharding import Mesh
from jax.sharding import PartitionSpec as P

HEAD_DIM = 64
GROUP_HEADS = 7
KV_GROUPS = 2
DP = ("dp_0", "dp_1", "dp_2")


rope_base = 1000000.0
norm_eps = 1e-06
sharpness_divisor = 0.05
objective_coefficient = 256.0


def laid_out(pieces, dim):
    pieces = jnp.moveaxis(pieces, 0, dim)
    lengths = pieces.shape
    return pieces.reshape(*lengths[:dim], lengths[dim] * lengths[dim + 1], *lengths[dim + 2 :])


def one_gather(arrays, axis, dims):
    vector = jnp.concatenate([a.reshape(-1) for a in arrays])
    lines, at, gathered = (lax.all_gather(vector, axis), 0, [])
    for a, dim in zip(arrays, dims):
        pieces = lines[:, at : at + a.size].reshape(-1, *a.shape)
        gathered.append(laid_out(pieces, dim))
        at += a.size
    return tuple(gathered)


def shifted(value, axis, steps):
    count = lax.axis_size(axis)
    first, last = (max(0, -steps), min(count, count - steps))
    return lax.ppermute(value, axis, [(source, source + steps) for source in range(first, last)])


def copy_for_each(shard, axis):
    copies = jnp.broadcast_to(shard, (lax.axis_size(axis), *shard.shape))
    return lax.all_to_all(copies, axis, split_axis=0, concat_axis=0, tiled=True)


def gathered_copies(shard, axis, dim):
    return laid_out(copy_for_each(shard, axis), dim)


def gathered_by_axis(shard, axes, dim):
    if not axes:
        return shard
    nearer = lax.all_gather(shard, axes[-1], axis=dim, tiled=True)
    return gathered_by_axis(nearer, axes[:-1], dim)


def rotary(values, positions):
    half_dim = values.shape[-1] // 2
    frequency = rope_base ** (-jnp.arange(half_dim, dtype=jnp.float32) * (2.0 / values.shape[-1]))
    angles = positions.astype(jnp.float32)[:, None] * frequency[None, :]
    cosine = jnp.cos(angles)[:, None, :]
    sine_part = jnp.sin(angles)[:, None, :]
    first_half = values[..., :half_dim]
    second_half = values[..., half_dim:]
    return jnp.concatenate(
        [
            first_half * cosine - second_half * sine_part,
            second_half * cosine + first_half * sine_part,
        ],
        axis=-1,
    )


def rms_scale(values, gain_row):
    return (
        values * lax.rsqrt(jnp.mean(values * values, axis=-1, keepdims=True) + norm_eps) * gain_row
    )


def attention_layer(hidden, seq_lengths, gain_row, weight_qkv, weight_out):
    row_count, row_width = hidden.shape
    seq_count = seq_lengths.shape[0]
    length = row_count // seq_count
    q_width = weight_out.shape[0]
    kv_width = KV_GROUPS * HEAD_DIM
    wide_in = hidden.astype(jnp.float32)
    normed = rms_scale(wide_in, gain_row).astype(jnp.bfloat16)
    projected = jnp.dot(normed, weight_qkv, preferred_element_type=jnp.float32)
    positions = jnp.arange(length, dtype=jnp.int32)
    query_rot = rotary(
        projected[:, :q_width].reshape(seq_count, length, KV_GROUPS * GROUP_HEADS, HEAD_DIM),
        positions,
    ).astype(jnp.bfloat16)
    key_rot = rotary(
        projected[:, q_width : q_width + kv_width].reshape(seq_count, length, KV_GROUPS, HEAD_DIM),
        positions,
    ).astype(jnp.bfloat16)
    value_rows = (
        projected[:, q_width + kv_width :]
        .reshape(seq_count, length, KV_GROUPS, HEAD_DIM)
        .astype(jnp.bfloat16)
    )
    query_grid = query_rot.reshape(seq_count, length, KV_GROUPS, GROUP_HEADS, HEAD_DIM)
    scores = jnp.einsum(
        "sqgzd,skgd->sgzqk", query_grid.astype(jnp.float32), key_rot.astype(jnp.float32)
    ) * HEAD_DIM ** (-0.5)
    key_live = positions[None, :] < seq_lengths[:, None]
    weights = jnp.where(key_live[:, None, None, None, :], jnp.exp(scores), 0.0)
    prob_low = (weights / jnp.sum(weights, axis=-1, keepdims=True)).astype(jnp.bfloat16)
    context = jnp.einsum(
        "sgzqk,skgd->sqgzd", prob_low.astype(jnp.float32), value_rows.astype(jnp.float32)
    ).astype(jnp.bfloat16)
    branch = jnp.dot(
        context.reshape(row_count, q_width), weight_out, preferred_element_type=jnp.float32
    )
    return (wide_in + branch).astype(jnp.bfloat16)


def embed_rows(rows_in, final_gain):
    pooled = rms_scale(rows_in.astype(jnp.float32), final_gain)
    return pooled * lax.rsqrt(jnp.sum(pooled * pooled, axis=-1, keepdims=True))


def pair_terms(question_representation, passage_representation, positive):
    match_raw_scores = jnp.dot(
        question_representation, passage_representation.T, preferred_element_type=jnp.float32
    ) * (1.0 / sharpness_divisor)
    weights = jnp.exp(match_raw_scores)
    normalized_exponential_odds = weights / jnp.sum(weights, axis=-1, keepdims=True)
    correct_target_column = (
        positive[:, None] == jnp.arange(passage_representation.shape[0], dtype=jnp.int32)[None, :]
    ).astype(jnp.float32)
    return (normalized_exponential_odds - correct_target_column) * (
        objective_coefficient / sharpness_divisor
    )


def per_device(entry, norm_gain, w_qkv, w_out, final_gain, lengths, positive):
    section_id = lax.axis_index("section")
    section_count = lax.axis_size("section")
    row_width = entry.shape[1]
    micro_count = positive.shape[0]
    rows_micro = entry.shape[0] // micro_count
    length = rows_micro // 2
    full_qkv, full_out = one_gather((w_qkv, w_out), DP, (1, 1))
    full_qkv = full_qkv[0]
    full_out = full_out[0]
    gain_row = norm_gain[0]
    tick_count = micro_count + section_count - 1

    def apply_layer(values, seq_lengths):
        return attention_layer(values, seq_lengths, gain_row, full_qkv, full_out)

    def pieces(micro_id):
        slot_id = jnp.clip(micro_id, 0, micro_count - 1)
        seq_lengths = lax.dynamic_slice_in_dim(lengths, slot_id * 2, 2, 0)
        return (slot_id, seq_lengths)

    zero_stack = jnp.zeros((micro_count, rows_micro, row_width), jnp.bfloat16)
    zero_block = jnp.zeros((rows_micro, row_width), jnp.bfloat16)

    def forward_tick(tick_id, state_in):
        inbox_buf, stash_buf, final_out = state_in
        micro_id = tick_id - section_id
        is_live = jnp.logical_and(micro_id >= 0, micro_id < micro_count)
        slot_id, seq_lengths = pieces(micro_id)
        fresh_rows = lax.dynamic_slice_in_dim(entry, slot_id * rows_micro, rows_micro, 0)
        current = jnp.where(section_id == 0, fresh_rows, inbox_buf)
        result = lax.cond(
            is_live, lambda values: apply_layer(values, seq_lengths), lambda values: values, current
        )
        stash_buf = lax.dynamic_update_index_in_dim(
            stash_buf, jnp.where(is_live, current, stash_buf[slot_id]), slot_id, 0
        )
        keep_top = jnp.logical_and(is_live, section_id == section_count - 1)
        final_out = lax.dynamic_update_index_in_dim(
            final_out, jnp.where(keep_top, result, final_out[slot_id]), slot_id, 0
        )
        inbox_buf = shifted(result, "section", 1)
        return (inbox_buf, stash_buf, final_out)

    _, stash_buf, final_out = lax.fori_loop(
        0, tick_count, forward_tick, (zero_block, zero_stack, zero_stack)
    )
    seq_grid = final_out.reshape(micro_count * 2, length, row_width)
    last_rows = jnp.take_along_axis(seq_grid, (lengths - 1)[:, None, None], axis=1)[:, 0]
    embedding, back_embed = jax.vjp(lambda rows_in: embed_rows(rows_in, final_gain), last_rows)
    emb_low = embedding.astype(jnp.bfloat16)
    question_representation = emb_low[0::2]
    passage_representation = emb_low[1::2]
    replica = lax.axis_index(DP)
    both_embed = gathered_copies(
        jnp.stack([question_representation, passage_representation]), DP, 1
    )
    pair_all = gathered_by_axis(positive, DP, 0)
    pair_coef = pair_terms(both_embed[0], both_embed[1], pair_all)
    grad_query_all = jnp.dot(pair_coef, both_embed[1].astype(jnp.float32))
    grad_doc_all = jnp.dot(pair_coef.T, both_embed[0].astype(jnp.float32))
    grad_query = lax.dynamic_slice_in_dim(grad_query_all, replica * micro_count, micro_count, 0)
    grad_doc = lax.dynamic_slice_in_dim(grad_doc_all, replica * micro_count, micro_count, 0)
    grad_emb = jnp.stack([grad_query, grad_doc], axis=1).reshape(micro_count * 2, row_width)
    grad_last = back_embed(grad_emb)[0]
    slot_hit = jnp.arange(length, dtype=jnp.int32)[None, :] == (lengths - 1)[:, None]
    seed_grad = jnp.where(slot_hit[:, :, None], grad_last[:, None, :], 0).reshape(
        micro_count, rows_micro, row_width
    )

    def backward_tick(tick_id, state_in):
        inbox_buf, grad_buf = state_in
        micro_id = tick_id - (section_count - 1 - section_id)
        is_live = jnp.logical_and(micro_id >= 0, micro_id < micro_count)
        slot_id, seq_lengths = pieces(micro_id)
        upstream = jnp.where(section_id == section_count - 1, seed_grad[slot_id], inbox_buf)

        def pull_back(operand):
            saved_rows, cotangent = operand
            _, back_layer = jax.vjp(lambda values: apply_layer(values, seq_lengths), saved_rows)
            return back_layer(cotangent)[0]

        downstream = lax.cond(
            is_live, pull_back, lambda operand: operand[1], (stash_buf[slot_id], upstream)
        )
        grad_buf = lax.dynamic_update_index_in_dim(
            grad_buf, jnp.where(is_live, downstream, grad_buf[slot_id]), slot_id, 0
        )
        inbox_buf = shifted(downstream, "section", -1)
        return (inbox_buf, grad_buf)

    _, grad_buf = lax.fori_loop(0, tick_count, backward_tick, (zero_block, zero_stack))
    return grad_buf.reshape(1, micro_count * rows_micro, row_width)


def solution(mesh):
    finer = Mesh(
        mesh.devices.reshape(mesh.shape["section"], 4, 4, 2), ("section", "dp_0", "dp_1", "dp_2")
    )
    in_specs = (
        P(DP, None),
        P("section", None),
        P("section", DP, None),
        P("section", DP, None),
        P(),
        P(DP),
        P(DP),
    )
    out_specs = P("section", DP, None)
    return jax.shard_map(
        per_device, mesh=finer, in_specs=in_specs, out_specs=out_specs, check_vma=False
    )
```

profile of v0, /device:TPU:1, one launch (start us, length us, event | category | flops | bytes accessed | tf_op | source)
XLA Modules:
  0.0 959.0 jit_solution(15289980668878995511)
XLA Ops:
  11.2 75.7 %all-gather.3.cloned.1.call-done = bf16[7340032]{0:T(1024)(128)(2,1)} async-done(((bf16[229376]{0:T(1024)(128)(2,1)}), bf16[7340032]{0:T(1024)(128)(2,1)}) %all-gather.3.cloned.1.call-update) | async-done | bytes 14680080 | tf_op jit(solution)/shard_map/all_gather | solution.py:27
  86.9 13.2 %reshape.548 = bf16[32,229376]{1,0:T(8,128)(2,1)} reshape(bf16[7340032]{0:T(1024)(128)(2,1)} %all-gather.3.cloned.1.call-done) | data formatting | bytes 29360128 | tf_op jit(solution)/shard_map/all_gather | solution.py:27
  122.0 12.2 %squeeze_reshape_transpose_reshape.7 = bf16[896,3584]{1,0:T(8,128)(2,1)} reshape(bf16[32,100352]{1,0:T(8,128)(2,1)} %slice.117) | data formatting | bytes 12845056 | tf_op jit(solution)/shard_map/squeeze;reshape;transpose;reshape | solution.py:147
  135.5 256.3 %while.35 = (s32[]{:T(128)}, bf16[96,3584]{1,0:T(8,128)(2,1)S(1)}, bf16[2,96,3584]{2,1,0:T(8,128)(2,1)S(1)}, bf16[2,96,3584]{2,1,0:T(8,128)(2,1)}, s32[]{:T(128)...) while((s32[]{:T(128)}, bf16[96,3584]{1,0:T(8,128)(2,1)S(1)}, ...), condition=%wide.region_5.6_spmd, body=%wide.region_0.5_spmd.sunk | while | flops 1431407872 | bytes 44450632 | solution.py:182
  137.3 17.4 %conditional.4 = (bf16[96,3584]{1,0:T(8,128)(2,1)S(1)}) conditional(s32[]{:T(128)} %convert_element_type.382, bf16[96,3584]{1,0:T(8,128)(2,1)S(1)} %get-tuple-element.840, (bf16[96,3584]{1,0:T(8,128)(2,1)S(1)}, f32[1,3584]{1,0:T(1,128)}, bf16[3584,1152]{1,0:T(8,128)(2,1)}, s32[]{:T(128)}, s32[4]{0:T(128)}, ...), branch_computations={%region_1.1_spmd, %region_2.4_spmd} | conditional | flops 1430375680 | bytes 22430102 | solution.py:169
  157.7 13.0 %collective-permute-done = bf16[96,3584]{1,0:T(8,128)(2,1)S(1)} collective-permute-done((bf16[96,3584]{1,0:T(8,128)(2,1)S(1)}, bf16[96,3584]{1,0:T(8,128)(2,1)S(1)}, u32[]{:S(2)}, u32[]{:S(2)}) %collective-permute-start) | collective-permute-done | bytes 688160 | tf_op jit(solution)/shard_map/while/body/eval_jaxpr/ppermute | solution.py:38
  172.3 17.4 %conditional.4 = (bf16[96,3584]{1,0:T(8,128)(2,1)S(1)}) conditional(s32[]{:T(128)} %convert_element_type.382, bf16[96,3584]{1,0:T(8,128)(2,1)S(1)} %get-tuple-element.840, (bf16[96,3584]{1,0:T(8,128)(2,1)S(1)}, f32[1,3584]{1,0:T(1,128)}, bf16[3584,1152]{1,0:T(8,128)(2,1)}, s32[]{:T(128)}, s32[4]{0:T(128)}, ...), branch_computations={%region_1.1_spmd, %region_2.4_spmd} | conditional | flops 1430375680 | bytes 22430102 | solution.py:169
  195.6 12.1 %collective-permute-done = bf16[96,3584]{1,0:T(8,128)(2,1)S(1)} collective-permute-done((bf16[96,3584]{1,0:T(8,128)(2,1)S(1)}, bf16[96,3584]{1,0:T(8,128)(2,1)S(1)}, u32[]{:S(2)}, u32[]{:S(2)}) %collective-permute-start) | collective-permute-done | bytes 688160 | tf_op jit(solution)/shard_map/while/body/eval_jaxpr/ppermute | solution.py:38
  209.2 21.5 %collective-permute-start = (bf16[96,3584]{1,0:T(8,128)(2,1)S(1)}, bf16[96,3584]{1,0:T(8,128)(2,1)S(1)}, u32[]{:S(2)}, u32[]{:S(2)}) collective-permute-start(bf16[96,3584]{1,0:T(8,128)(2,1)S(1)} %get-tuple-element.946), channel_id=1, source_target_pairs={{0,32},{32,64},{64,96},{96,128},{128,160},{160,192},{192,224},{1,3... | collective-permute-start | bytes 2064392 | tf_op jit(solution)/shard_map/while/body/eval_jaxpr/ppermute | solution.py:38
  232.5 11.3 %collective-permute-done = bf16[96,3584]{1,0:T(8,128)(2,1)S(1)} collective-permute-done((bf16[96,3584]{1,0:T(8,128)(2,1)S(1)}, bf16[96,3584]{1,0:T(8,128)(2,1)S(1)}, u32[]{:S(2)}, u32[]{:S(2)}) %collective-permute-start) | collective-permute-done | bytes 688160 | tf_op jit(solution)/shard_map/while/body/eval_jaxpr/ppermute | solution.py:38
  251.2 10.4 %collective-permute-done = bf16[96,3584]{1,0:T(8,128)(2,1)S(1)} collective-permute-done((bf16[96,3584]{1,0:T(8,128)(2,1)S(1)}, bf16[96,3584]{1,0:T(8,128)(2,1)S(1)}, u32[]{:S(2)}, u32[]{:S(2)}) %collective-permute-start) | collective-permute-done | bytes 688160 | tf_op jit(solution)/shard_map/while/body/eval_jaxpr/ppermute | solution.py:38
  263.1 20.2 %collective-permute-start = (bf16[96,3584]{1,0:T(8,128)(2,1)S(1)}, bf16[96,3584]{1,0:T(8,128)(2,1)S(1)}, u32[]{:S(2)}, u32[]{:S(2)}) collective-permute-start(bf16[96,3584]{1,0:T(8,128)(2,1)S(1)} %get-tuple-element.946), channel_id=1, source_target_pairs={{0,32},{32,64},{64,96},{96,128},{128,160},{160,192},{192,224},{1,3... | collective-permute-start | bytes 2064392 | tf_op jit(solution)/shard_map/while/body/eval_jaxpr/ppermute | solution.py:38
  312.8 20.4 %collective-permute-start = (bf16[96,3584]{1,0:T(8,128)(2,1)S(1)}, bf16[96,3584]{1,0:T(8,128)(2,1)S(1)}, u32[]{:S(2)}, u32[]{:S(2)}) collective-permute-start(bf16[96,3584]{1,0:T(8,128)(2,1)S(1)} %get-tuple-element.946), channel_id=1, source_target_pairs={{0,32},{32,64},{64,96},{96,128},{128,160},{160,192},{192,224},{1,3... | collective-permute-start | bytes 2064392 | tf_op jit(solution)/shard_map/while/body/eval_jaxpr/ppermute | solution.py:38
  359.9 23.2 %collective-permute-start = (bf16[96,3584]{1,0:T(8,128)(2,1)S(1)}, bf16[96,3584]{1,0:T(8,128)(2,1)S(1)}, u32[]{:S(2)}, u32[]{:S(2)}) collective-permute-start(bf16[96,3584]{1,0:T(8,128)(2,1)S(1)} %get-tuple-element.946), channel_id=1, source_target_pairs={{0,32},{32,64},{64,96},{96,128},{128,160},{160,192},{192,224},{1,3... | collective-permute-start | bytes 2064392 | tf_op jit(solution)/shard_map/while/body/eval_jaxpr/ppermute | solution.py:38
  395.6 12.0 %all-to-all-start = ((bf16[32,2,2,3584]{3,2,1,0:T(2,128)(2,1)}), bf16[32,2,2,3584]{3,2,1,0:T(2,128)(2,1)S(1)}, u32[]{:S(2)}, u32[]{:S(2)}) async-start(bf16[32,2,2,3584]{3,2,1,0:T(2,128)(2,1)} %broadcast_in_dim.167), calls=%async_computation | async-start | bytes 1835008 | tf_op jit(solution)/shard_map/all_to_all | solution.py:43
  435.4 516.8 %while.36 = (s32[]{:T(128)}, bf16[96,3584]{1,0:T(8,128)(2,1)S(1)}, bf16[2,96,3584]{2,1,0:T(8,128)(2,1)}, s32[]{:T(128)}, pred[]{:T(512)}, /*index=5*/bf16[2,96,3...) while((s32[]{:T(128)}, bf16[96,3584]{1,0:T(8,128)(2,1)S(1)}, ...), condition=%wide.region_18.19_spmd, body=%wide.region_11.18_spmd.sunk | while | flops 2254882304 | bytes 64684780 | solution.py:229
  439.9 14.5 %collective-permute-done.1 = bf16[96,3584]{1,0:T(8,128)(2,1)S(1)} collective-permute-done((bf16[96,3584]{1,0:T(8,128)(2,1)S(1)}, bf16[96,3584]{1,0:T(8,128)(2,1)S(1)}, u32[]{:S(2)}, u32[]{:S(2)}) %collective-permute-start.1) | collective-permute-done | bytes 688160 | tf_op jit(solution)/shard_map/while/body/eval_jaxpr/ppermute | solution.py:38
  458.6 27.6 %collective-permute-done.1 = bf16[96,3584]{1,0:T(8,128)(2,1)S(1)} collective-permute-done((bf16[96,3584]{1,0:T(8,128)(2,1)S(1)}, bf16[96,3584]{1,0:T(8,128)(2,1)S(1)}, u32[]{:S(2)}, u32[]{:S(2)}) %collective-permute-start.1) | collective-permute-done | bytes 688160 | tf_op jit(solution)/shard_map/while/body/eval_jaxpr/ppermute | solution.py:38
  490.4 13.4 %collective-permute-done.1 = bf16[96,3584]{1,0:T(8,128)(2,1)S(1)} collective-permute-done((bf16[96,3584]{1,0:T(8,128)(2,1)S(1)}, bf16[96,3584]{1,0:T(8,128)(2,1)S(1)}, u32[]{:S(2)}, u32[]{:S(2)}) %collective-permute-start.1) | collective-permute-done | bytes 688160 | tf_op jit(solution)/shard_map/while/body/eval_jaxpr/ppermute | solution.py:38
  508.0 26.2 %collective-permute-done.1 = bf16[96,3584]{1,0:T(8,128)(2,1)S(1)} collective-permute-done((bf16[96,3584]{1,0:T(8,128)(2,1)S(1)}, bf16[96,3584]{1,0:T(8,128)(2,1)S(1)}, u32[]{:S(2)}, u32[]{:S(2)}) %collective-permute-start.1) | collective-permute-done | bytes 688160 | tf_op jit(solution)/shard_map/while/body/eval_jaxpr/ppermute | solution.py:38
  553.0 26.5 %collective-permute-done.1 = bf16[96,3584]{1,0:T(8,128)(2,1)S(1)} collective-permute-done((bf16[96,3584]{1,0:T(8,128)(2,1)S(1)}, bf16[96,3584]{1,0:T(8,128)(2,1)S(1)}, u32[]{:S(2)}, u32[]{:S(2)}) %collective-permute-start.1) | collective-permute-done | bytes 688160 | tf_op jit(solution)/shard_map/while/body/eval_jaxpr/ppermute | solution.py:38
  583.8 268.3 %collective-permute-done.1 = bf16[96,3584]{1,0:T(8,128)(2,1)S(1)} collective-permute-done((bf16[96,3584]{1,0:T(8,128)(2,1)S(1)}, bf16[96,3584]{1,0:T(8,128)(2,1)S(1)}, u32[]{:S(2)}, u32[]{:S(2)}) %collective-permute-start.1) | collective-permute-done | bytes 688160 | tf_op jit(solution)/shard_map/while/body/eval_jaxpr/ppermute | solution.py:38
  853.3 37.0 %conditional.5 = (bf16[96,3584]{1,0:T(8,128)(2,1)S(1)}) conditional(s32[]{:T(128)} %convert_element_type.383, bf16[96,3584]{1,0:T(8,128)(2,1)S(1)} %bitcast_select_fusion.7, (bf16[96,3584]{1,0:T(8,128)(2,1)S(1)}, bf16[896,3584]{1,0:T(8,128)(2,1)}, s32[]{:T(128)}, s32[4]{0:T(128)}, bf16[2,96,3584]{2,1,0:T(8,128)(2,1)S(1)}, ...), branch_computations={%region_12.12_spmd, %region_13.17_spmd} | conditional | flops 2254194176 | bytes 45416836 | solution.py:220
  903.4 37.0 %conditional.5 = (bf16[96,3584]{1,0:T(8,128)(2,1)S(1)}) conditional(s32[]{:T(128)} %convert_element_type.383, bf16[96,3584]{1,0:T(8,128)(2,1)S(1)} %bitcast_select_fusion.7, (bf16[96,3584]{1,0:T(8,128)(2,1)S(1)}, bf16[896,3584]{1,0:T(8,128)(2,1)}, s32[]{:T(128)}, s32[4]{0:T(128)}, bf16[2,96,3584]{2,1,0:T(8,128)(2,1)S(1)}, ...), branch_computations={%region_12.12_spmd, %region_13.17_spmd} | conditional | flops 2254194176 | bytes 45416836 | solution.py:220
  (449 shorter events, 319.1 us)
Async XLA Ops:
  6.5 80.4 %all-gather.3.cloned.1.call-start = ((), (), s32[]{:S(2)}) async-start(), calls=%async_computation.1 | async-start | bytes 15138816 | tf_op jit(solution)/shard_map/all_gather | solution.py:27
  135.5 258.1 %copy-start.15 = (f32[3584]{0:T(1024)S(1)}, f32[3584]{0:T(1024)}, u32[]{:S(2)}) copy-start(f32[3584]{0:T(1024)} %param.19) | copy-start | bytes 43012
  154.7 16.1 %collective-permute-start = (bf16[96,3584]{1,0:T(8,128)(2,1)S(1)}, bf16[96,3584]{1,0:T(8,128)(2,1)S(1)}, u32[]{:S(2)}, u32[]{:S(2)}) collective-permute-start(bf16[96,3584]{1,0:T(8,128)(2,1)S(1)} %get-tuple-element.946), channel_id=1, source_target_pairs={{0,32},{32,64},{64,96},{96,128},{128,160},{160,192},{192,224},{1,3... | collective-permute-start | bytes 2064392 | tf_op jit(solution)/shard_map/while/body/eval_jaxpr/ppermute | solution.py:38
  189.7 18.0 %collective-permute-start = (bf16[96,3584]{1,0:T(8,128)(2,1)S(1)}, bf16[96,3584]{1,0:T(8,128)(2,1)S(1)}, u32[]{:S(2)}, u32[]{:S(2)}) collective-permute-start(bf16[96,3584]{1,0:T(8,128)(2,1)S(1)} %get-tuple-element.946), channel_id=1, source_target_pairs={{0,32},{32,64},{64,96},{96,128},{128,160},{160,192},{192,224},{1,3... | collective-permute-start | bytes 2064392 | tf_op jit(solution)/shard_map/while/body/eval_jaxpr/ppermute | solution.py:38
  209.2 34.6 %collective-permute-start = (bf16[96,3584]{1,0:T(8,128)(2,1)S(1)}, bf16[96,3584]{1,0:T(8,128)(2,1)S(1)}, u32[]{:S(2)}, u32[]{:S(2)}) collective-permute-start(bf16[96,3584]{1,0:T(8,128)(2,1)S(1)} %get-tuple-element.946), channel_id=1, source_target_pairs={{0,32},{32,64},{64,96},{96,128},{128,160},{160,192},{192,224},{1,3... | collective-permute-start | bytes 2064392 | tf_op jit(solution)/shard_map/while/body/eval_jaxpr/ppermute | solution.py:38
  245.3 16.3 %collective-permute-start = (bf16[96,3584]{1,0:T(8,128)(2,1)S(1)}, bf16[96,3584]{1,0:T(8,128)(2,1)S(1)}, u32[]{:S(2)}, u32[]{:S(2)}) collective-permute-start(bf16[96,3584]{1,0:T(8,128)(2,1)S(1)} %get-tuple-element.946), channel_id=1, source_target_pairs={{0,32},{32,64},{64,96},{96,128},{128,160},{160,192},{192,224},{1,3... | collective-permute-start | bytes 2064392 | tf_op jit(solution)/shard_map/while/body/eval_jaxpr/ppermute | solution.py:38
  263.1 31.8 %collective-permute-start = (bf16[96,3584]{1,0:T(8,128)(2,1)S(1)}, bf16[96,3584]{1,0:T(8,128)(2,1)S(1)}, u32[]{:S(2)}, u32[]{:S(2)}) collective-permute-start(bf16[96,3584]{1,0:T(8,128)(2,1)S(1)} %get-tuple-element.946), channel_id=1, source_target_pairs={{0,32},{32,64},{64,96},{96,128},{128,160},{160,192},{192,224},{1,3... | collective-permute-start | bytes 2064392 | tf_op jit(solution)/shard_map/while/body/eval_jaxpr/ppermute | solution.py:38
  296.4 14.9 %collective-permute-start = (bf16[96,3584]{1,0:T(8,128)(2,1)S(1)}, bf16[96,3584]{1,0:T(8,128)(2,1)S(1)}, u32[]{:S(2)}, u32[]{:S(2)}) collective-permute-start(bf16[96,3584]{1,0:T(8,128)(2,1)S(1)} %get-tuple-element.946), channel_id=1, source_target_pairs={{0,32},{32,64},{64,96},{96,128},{128,160},{160,192},{192,224},{1,3... | collective-permute-start | bytes 2064392 | tf_op jit(solution)/shard_map/while/body/eval_jaxpr/ppermute | solution.py:38
  312.8 30.6 %collective-permute-start = (bf16[96,3584]{1,0:T(8,128)(2,1)S(1)}, bf16[96,3584]{1,0:T(8,128)(2,1)S(1)}, u32[]{:S(2)}, u32[]{:S(2)}) collective-permute-start(bf16[96,3584]{1,0:T(8,128)(2,1)S(1)} %get-tuple-element.946), channel_id=1, source_target_pairs={{0,32},{32,64},{64,96},{96,128},{128,160},{160,192},{192,224},{1,3... | collective-permute-start | bytes 2064392 | tf_op jit(solution)/shard_map/while/body/eval_jaxpr/ppermute | solution.py:38
  344.9 13.4 %collective-permute-start = (bf16[96,3584]{1,0:T(8,128)(2,1)S(1)}, bf16[96,3584]{1,0:T(8,128)(2,1)S(1)}, u32[]{:S(2)}, u32[]{:S(2)}) collective-permute-start(bf16[96,3584]{1,0:T(8,128)(2,1)S(1)} %get-tuple-element.946), channel_id=1, source_target_pairs={{0,32},{32,64},{64,96},{96,128},{128,160},{160,192},{192,224},{1,3... | collective-permute-start | bytes 2064392 | tf_op jit(solution)/shard_map/while/body/eval_jaxpr/ppermute | solution.py:38
  359.9 31.9 %collective-permute-start = (bf16[96,3584]{1,0:T(8,128)(2,1)S(1)}, bf16[96,3584]{1,0:T(8,128)(2,1)S(1)}, u32[]{:S(2)}, u32[]{:S(2)}) collective-permute-start(bf16[96,3584]{1,0:T(8,128)(2,1)S(1)} %get-tuple-element.946), channel_id=1, source_target_pairs={{0,32},{32,64},{64,96},{96,128},{128,160},{160,192},{192,224},{1,3... | collective-permute-start | bytes 2064392 | tf_op jit(solution)/shard_map/while/body/eval_jaxpr/ppermute | solution.py:38
  395.6 34.5 %all-to-all-start = ((bf16[32,2,2,3584]{3,2,1,0:T(2,128)(2,1)}), bf16[32,2,2,3584]{3,2,1,0:T(2,128)(2,1)S(1)}, u32[]{:S(2)}, u32[]{:S(2)}) async-start(bf16[32,2,2,3584]{3,2,1,0:T(2,128)(2,1)} %broadcast_in_dim.167), calls=%async_computation | async-start | bytes 1835008 | tf_op jit(solution)/shard_map/all_to_all | solution.py:43
  436.8 17.6 %collective-permute-start.1 = (bf16[96,3584]{1,0:T(8,128)(2,1)S(1)}, bf16[96,3584]{1,0:T(8,128)(2,1)S(1)}, u32[]{:S(2)}, u32[]{:S(2)}) collective-permute-start(bf16[96,3584]{1,0:T(8,128)(2,1)S(1)} %get-tuple-element.947), channel_id=1, source_target_pairs={{32,0},{64,32},{96,64},{128,96},{160,128},{192,160},{224,192},{33,... | collective-permute-start | bytes 2064392 | tf_op jit(solution)/shard_map/while/body/eval_jaxpr/ppermute | solution.py:38
  455.6 30.6 %collective-permute-start.1 = (bf16[96,3584]{1,0:T(8,128)(2,1)S(1)}, bf16[96,3584]{1,0:T(8,128)(2,1)S(1)}, u32[]{:S(2)}, u32[]{:S(2)}) collective-permute-start(bf16[96,3584]{1,0:T(8,128)(2,1)S(1)} %get-tuple-element.947), channel_id=1, source_target_pairs={{32,0},{64,32},{96,64},{128,96},{160,128},{192,160},{224,192},{33,... | collective-permute-start | bytes 2064392 | tf_op jit(solution)/shard_map/while/body/eval_jaxpr/ppermute | solution.py:38
  458.6 27.6 %copy-start.8 = (bf16[2,96,3584]{2,1,0:T(8,128)(2,1)}, bf16[2,96,3584]{2,1,0:T(8,128)(2,1)S(1)}, u32[]{:S(2)}) copy-start(bf16[2,96,3584]{2,1,0:T(8,128)(2,1)S(1)} %bitcast_dynamic-update-slice_fusion.8) | copy-start | bytes 4128772 | tf_op jit(solution)/shard_map/while
  487.4 16.4 %collective-permute-start.1 = (bf16[96,3584]{1,0:T(8,128)(2,1)S(1)}, bf16[96,3584]{1,0:T(8,128)(2,1)S(1)}, u32[]{:S(2)}, u32[]{:S(2)}) collective-permute-start(bf16[96,3584]{1,0:T(8,128)(2,1)S(1)} %get-tuple-element.947), channel_id=1, source_target_pairs={{32,0},{64,32},{96,64},{128,96},{160,128},{192,160},{224,192},{33,... | collective-permute-start | bytes 2064392 | tf_op jit(solution)/shard_map/while/body/eval_jaxpr/ppermute | solution.py:38
  505.0 29.2 %collective-permute-start.1 = (bf16[96,3584]{1,0:T(8,128)(2,1)S(1)}, bf16[96,3584]{1,0:T(8,128)(2,1)S(1)}, u32[]{:S(2)}, u32[]{:S(2)}) collective-permute-start(bf16[96,3584]{1,0:T(8,128)(2,1)S(1)} %get-tuple-element.947), channel_id=1, source_target_pairs={{32,0},{64,32},{96,64},{128,96},{160,128},{192,160},{224,192},{33,... | collective-permute-start | bytes 2064392 | tf_op jit(solution)/shard_map/while/body/eval_jaxpr/ppermute | solution.py:38
  535.4 13.4 %collective-permute-start.1 = (bf16[96,3584]{1,0:T(8,128)(2,1)S(1)}, bf16[96,3584]{1,0:T(8,128)(2,1)S(1)}, u32[]{:S(2)}, u32[]{:S(2)}) collective-permute-start(bf16[96,3584]{1,0:T(8,128)(2,1)S(1)} %get-tuple-element.947), channel_id=1, source_target_pairs={{32,0},{64,32},{96,64},{128,96},{160,128},{192,160},{224,192},{33,... | collective-permute-start | bytes 2064392 | tf_op jit(solution)/shard_map/while/body/eval_jaxpr/ppermute | solution.py:38
  550.0 29.6 %collective-permute-start.1 = (bf16[96,3584]{1,0:T(8,128)(2,1)S(1)}, bf16[96,3584]{1,0:T(8,128)(2,1)S(1)}, u32[]{:S(2)}, u32[]{:S(2)}) collective-permute-start(bf16[96,3584]{1,0:T(8,128)(2,1)S(1)} %get-tuple-element.947), channel_id=1, source_target_pairs={{32,0},{64,32},{96,64},{128,96},{160,128},{192,160},{224,192},{33,... | collective-permute-start | bytes 2064392 | tf_op jit(solution)/shard_map/while/body/eval_jaxpr/ppermute | solution.py:38
  553.0 26.6 %copy-start.8 = (bf16[2,96,3584]{2,1,0:T(8,128)(2,1)}, bf16[2,96,3584]{2,1,0:T(8,128)(2,1)S(1)}, u32[]{:S(2)}) copy-start(bf16[2,96,3584]{2,1,0:T(8,128)(2,1)S(1)} %bitcast_dynamic-update-slice_fusion.8) | copy-start | bytes 4128772 | tf_op jit(solution)/shard_map/while
  580.8 271.3 %collective-permute-start.1 = (bf16[96,3584]{1,0:T(8,128)(2,1)S(1)}, bf16[96,3584]{1,0:T(8,128)(2,1)S(1)}, u32[]{:S(2)}, u32[]{:S(2)}) collective-permute-start(bf16[96,3584]{1,0:T(8,128)(2,1)S(1)} %get-tuple-element.947), channel_id=1, source_target_pairs={{32,0},{64,32},{96,64},{128,96},{160,128},{192,160},{224,192},{33,... | collective-permute-start | bytes 2064392 | tf_op jit(solution)/shard_map/while/body/eval_jaxpr/ppermute | solution.py:38
  583.8 268.3 %copy-start.8 = (bf16[2,96,3584]{2,1,0:T(8,128)(2,1)}, bf16[2,96,3584]{2,1,0:T(8,128)(2,1)S(1)}, u32[]{:S(2)}) copy-start(bf16[2,96,3584]{2,1,0:T(8,128)(2,1)S(1)} %bitcast_dynamic-update-slice_fusion.8) | copy-start | bytes 4128772 | tf_op jit(solution)/shard_map/while
  890.3 11.9 %collective-permute-start.1 = (bf16[96,3584]{1,0:T(8,128)(2,1)S(1)}, bf16[96,3584]{1,0:T(8,128)(2,1)S(1)}, u32[]{:S(2)}, u32[]{:S(2)}) collective-permute-start(bf16[96,3584]{1,0:T(8,128)(2,1)S(1)} %get-tuple-element.947), channel_id=1, source_target_pairs={{32,0},{64,32},{96,64},{128,96},{160,128},{192,160},{224,192},{33,... | collective-permute-start | bytes 2064392 | tf_op jit(solution)/shard_map/while/body/eval_jaxpr/ppermute | solution.py:38
  940.4 11.7 %collective-permute-start.1 = (bf16[96,3584]{1,0:T(8,128)(2,1)S(1)}, bf16[96,3584]{1,0:T(8,128)(2,1)S(1)}, u32[]{:S(2)}, u32[]{:S(2)}) collective-permute-start(bf16[96,3584]{1,0:T(8,128)(2,1)S(1)} %get-tuple-element.947), channel_id=1, source_target_pairs={{32,0},{64,32},{96,64},{128,96},{160,128},{192,160},{224,192},{33,... | collective-permute-start | bytes 2064392 | tf_op jit(solution)/shard_map/while/body/eval_jaxpr/ppermute | solution.py:38
  (71 other events, 350.5 us)
Sparse Core Ops, SparseCore 0:
  9.9 76.9 all-gather.2
where the time goes:
time: 974 us; the launch traced here: 959 us
  waiting for transfers between devices  569 us (58%)
  starting transfers between devices  127 us (13%)
  local copies, waits for them, and re-layouts  113 us (12%)
  matrix products  71.1 us (7%)
  other arithmetic  43.3 us (4%)
  blocking collectives  17.5 us (2%)
  between operations  15.6 us (2%)
    ppermute x18, waiting for transfers between devices, shifted(): lax.ppermute(value, axis, [(source, source + steps) for source in range(f...  493 us
    ppermute x18, starting transfers between devices, shifted(): lax.ppermute(value, axis, [(source, source + steps) for source in range(f...  115 us
    all_gather x1, waiting for transfers between devices, one_gather(): lines, at, gathered = (lax.all_gather(vector, axis), 0, [])  75.7 us
    dot_general x6, matrix products, attention_layer(): projected = jnp.dot(normed, weight_qkv, preferred_element_type=jnp.float32)  31.7 us
  transfers between devices with their start and end apart: 20, of which 19 were waited for; matrix products, arithmetic and copies ran while one was open for 3% of the time, Pallas kernels for 0%

commit v1 on v0

v1 whole, which is shorter than its diff:
```python
import functools

import jax
import jax.numpy as jnp
from jax import lax
from jax.experimental import pallas as pl
from jax.experimental.pallas import tpu as pltpu
from jax.sharding import Mesh
from jax.sharding import PartitionSpec as P

HEAD_DIM = 64
LEN = 48
D = 3584
QW = 896
KV = 128
XW = QW + 2 * KV
PACK = XW + QW
PAIRS = QW // 128
DP = ("dp_0", "dp_1", "dp_2")
ROPE_BASE = 1000000.0
EPS = 1e-06
SHARP = 20.0
COEF = 256.0
CHUNK = 512
CHUNKS = D // CHUNK
F32 = jnp.float32
BF16 = jnp.bfloat16


def dot_nn(a, b):
    return lax.dot_general(a, b, (((1,), (0,)), ((), ())), preferred_element_type=F32)


def dot_nt(a, b):
    return lax.dot_general(a, b, (((1,), (1,)), ((), ())), preferred_element_type=F32)


def dot_tn(a, b):
    return lax.dot_general(a, b, (((0,), (0,)), ((), ())), preferred_element_type=F32)


def lanes(rows):
    return lax.broadcasted_iota(jnp.int32, (rows, 128), 1)


def partner(x):
    low = lax.rem(lanes(x.shape[0]), 64) < 32
    return jnp.where(low, pltpu.roll(x, 96, 1), pltpu.roll(x, 32, 1))


def paired(z):
    left = lanes(LEN) < 64
    rolled = pltpu.roll(z, 64, 1)
    pad = jnp.zeros((16, 128), BF16)
    a_left = jnp.where(left, z, 0.0).astype(BF16)
    b_right = jnp.where(left, 0.0, z).astype(BF16)
    b_left = jnp.where(left, rolled, 0.0).astype(BF16)
    a_right = jnp.where(left, 0.0, rolled).astype(BF16)
    return (
        jnp.concatenate([a_left, pad, a_right, pad], axis=0),
        jnp.concatenate([a_left, pad, b_right, pad], axis=0),
        jnp.concatenate([b_left, pad, b_right, pad], axis=0),
    )


SPANS = ((0, 3 * LEN), (3 * LEN, 4 * LEN), (4 * LEN, 7 * LEN))


def by_pair(dot, rows, blocks):
    return jnp.concatenate(
        [dot(rows[lo:hi], block) for (lo, hi), block in zip(SPANS, blocks)], axis=0
    )


def unpaired(rows, other):
    left = lanes(LEN) < 64
    s00, s01, s11 = (dot_tn(rows[lo:hi], other[lo:hi]) for lo, hi in SPANS)
    first = jnp.where(left, s00[:LEN] + s01[:LEN], 0.0)
    first += pltpu.roll(jnp.where(left, 0.0, s00[64 : 64 + LEN]), 64, 1)
    second = jnp.where(left, 0.0, s01[64 : 64 + LEN] + s11[64 : 64 + LEN])
    second += pltpu.roll(jnp.where(left, s11[:LEN], 0.0), 64, 1)
    return first + second


def half_sums(x):
    left = lanes(x.shape[0]) < 64
    low = jnp.sum(jnp.where(left, x, 0.0), axis=1, keepdims=True)
    high = jnp.sum(jnp.where(left, 0.0, x), axis=1, keepdims=True)
    return low, high, left


def probabilities(q_rows, k_blocks, length):
    scores = by_pair(dot_nt, q_rows, k_blocks) * HEAD_DIM ** (-0.5)
    live = lax.rem(lanes(scores.shape[0]), 64) < length
    weights = jnp.where(live, jnp.exp(scores), 0.0)
    low, high, left = half_sums(weights)
    return weights * jnp.where(left, 1.0 / low, 1.0 / high)


def rows_of(x_ref):
    return jnp.concatenate([x_ref[:, 128 * i : 128 * i + 128] for i in range(PAIRS)], axis=0)


def inv_rms(wide):
    return lax.rsqrt(jnp.sum(wide * wide, axis=1, keepdims=True) * (1.0 / D) + EPS)


def forward_kernel(
    tick,
    last_stage,
    micro,
    meta,
    inbox,
    entry,
    gain,
    table,
    packed,
    w_out,
    stash_h_in,
    stash_x_in,
    last_in,
    out,
    stash_h,
    stash_x,
    last,
    wq_v,
    wo_v,
    h_v,
    n_v,
    acc_v,
    x_v,
    ctx_v,
    last_v,
    wq_sem,
    wo_sem,
    sems,
):
    del stash_h_in, stash_x_in, last_in
    stage = meta[0]
    slot = tick - stage

    @pl.when(jnp.logical_and(slot >= 0, slot < micro))
    def _():
        length = meta[1 + slot]
        row0 = pl.multiple_of(slot * LEN, LEN)

        def wq_copy(i):
            rows = pl.ds(pl.multiple_of(i * CHUNK, CHUNK), CHUNK)
            return pltpu.make_async_copy(
                packed.at[rows, pl.ds(0, XW)], wq_v.at[rows, :], wq_sem.at[i]
            )

        def wo_copy(i):
            cols = pl.ds(pl.multiple_of(i * CHUNK, CHUNK), CHUNK)
            return pltpu.make_async_copy(w_out.at[:, cols], wo_v.at[:, cols], wo_sem.at[i])

        first = pltpu.make_async_copy(entry.at[pl.ds(row0, LEN), :], h_v, sems.at[0])
        later = pltpu.make_async_copy(inbox, h_v, sems.at[0])

        @pl.when(stage == 0)
        def _():
            first.start()

        @pl.when(stage != 0)
        def _():
            later.start()

        for i in range(CHUNKS):
            wq_copy(i).start()
        for i in range(CHUNKS):
            wo_copy(i).start()
        later.wait()
        keep_h = pltpu.make_async_copy(h_v, stash_h.at[pl.ds(row0, LEN), :], sems.at[1])
        keep_h.start()
        wide = h_v[...].astype(F32)
        n_v[...] = (wide * inv_rms(wide) * gain[...]).astype(BF16)
        acc_v[...] = jnp.zeros_like(acc_v)

        @pl.loop(0, CHUNKS)
        def _(i):
            wq_copy(i).wait()
            cols = pl.ds(pl.multiple_of(i * CHUNK, CHUNK), CHUNK)
            acc_v[...] += dot_nn(n_v[:, cols], wq_v[cols, :])

        cosine, sine = table[0], table[1]
        for i in range(PAIRS + 1):
            part = acc_v[:, 128 * i : 128 * i + 128]
            x_v[:, 128 * i : 128 * i + 128] = (part * cosine + partner(part) * sine).astype(BF16)
        x_v[:, QW + KV :] = acc_v[:, QW + KV :].astype(BF16)
        keep_x = pltpu.make_async_copy(x_v, stash_x.at[pl.ds(row0, LEN), :], sems.at[2])
        keep_x.start()
        k_blocks = paired(x_v[:, QW : QW + KV].astype(F32))
        v_blocks = paired(x_v[:, QW + KV :].astype(F32))
        probs = probabilities(rows_of(x_v), k_blocks, length).astype(BF16)
        context = by_pair(dot_nn, probs, v_blocks).astype(BF16)
        for i in range(PAIRS):
            ctx_v[:, 128 * i : 128 * i + 128] = context[LEN * i : LEN * i + LEN]

        @pl.loop(0, CHUNKS)
        def _(i):
            wo_copy(i).wait()
            cols = pl.ds(pl.multiple_of(i * CHUNK, CHUNK), CHUNK)
            branch = dot_nn(ctx_v[...], wo_v[:, cols])
            out[:, cols] = (h_v[:, cols].astype(F32) + branch).astype(BF16)

        @pl.when(stage == last_stage)
        def _():
            hit = lax.broadcasted_iota(jnp.int32, (LEN, D), 0) == length - 1
            row = jnp.sum(jnp.where(hit, out[...].astype(F32), 0.0), axis=0, keepdims=True)
            last_v[...] = jnp.broadcast_to(row, (8, D))
            put = pltpu.make_async_copy(last_v, last.at[slot], sems.at[3])
            put.start()
            put.wait()

        keep_h.wait()
        keep_x.wait()


def backward_kernel(
    tick,
    last_stage,
    micro,
    meta,
    inbox,
    seed,
    gain,
    table,
    packed,
    w_out,
    stash_h,
    stash_x,
    grads_in,
    out,
    grads,
    wq_v,
    wo_v,
    h_v,
    g_v,
    x_v,
    dctx_v,
    dx_v,
    dn_v,
    wq_sem,
    wo_sem,
    sems,
):
    del grads_in
    stage = meta[0]
    slot = tick - (last_stage - stage)

    @pl.when(jnp.logical_and(slot >= 0, slot < micro))
    def _():
        length = meta[1 + slot]
        row0 = pl.multiple_of(slot * LEN, LEN)

        def wq_copy(i):
            rows = pl.ds(pl.multiple_of(i * CHUNK, CHUNK), CHUNK)
            return pltpu.make_async_copy(
                packed.at[rows, pl.ds(0, XW)], wq_v.at[rows, :], wq_sem.at[i]
            )

        def wo_copy(i):
            cols = pl.ds(pl.multiple_of(i * CHUNK, CHUNK), CHUNK)
            return pltpu.make_async_copy(w_out.at[:, cols], wo_v.at[:, cols], wo_sem.at[i])

        for i in range(CHUNKS):
            wo_copy(i).start()
        get_x = pltpu.make_async_copy(stash_x.at[pl.ds(row0, LEN), :], x_v, sems.at[0])
        get_h = pltpu.make_async_copy(stash_h.at[pl.ds(row0, LEN), :], h_v, sems.at[1])
        get_x.start()
        get_h.start()
        for i in range(CHUNKS):
            wq_copy(i).start()

        @pl.when(stage == last_stage)
        def _():
            hit = lax.broadcasted_iota(jnp.int32, (LEN, D), 0) == length - 1
            row = jnp.where(lax.broadcasted_iota(jnp.int32, (8, D), 0) == slot, seed[...], 0.0)
            row = jnp.sum(row, axis=0, keepdims=True)
            g_v[...] = jnp.where(hit, jnp.broadcast_to(row, (LEN, D)), 0.0).astype(BF16)

        @pl.when(stage != last_stage)
        def _():
            g_v[...] = inbox[...]

        dctx_v[...] = jnp.zeros_like(dctx_v)

        @pl.loop(0, CHUNKS)
        def _(i):
            wo_copy(i).wait()
            cols = pl.ds(pl.multiple_of(i * CHUNK, CHUNK), CHUNK)
            dctx_v[...] += dot_nt(g_v[:, cols], wo_v[:, cols])

        get_x.wait()
        q_rows = rows_of(x_v)
        k_blocks = paired(x_v[:, QW : QW + KV].astype(F32))
        v_blocks = paired(x_v[:, QW + KV :].astype(F32))
        probs = probabilities(q_rows, k_blocks, length)
        dctx = rows_of(dctx_v).astype(BF16)
        dvalue = unpaired(probs.astype(BF16), dctx)
        dprobs = by_pair(dot_nt, dctx, v_blocks).astype(BF16).astype(F32)
        low, high, left = half_sums(dprobs * probs)
        dscores = probs * (dprobs - jnp.where(left, low, high)) * HEAD_DIM ** (-0.5)
        dscores = dscores.astype(BF16)
        dquery = by_pair(dot_nn, dscores, k_blocks).astype(BF16).astype(F32)
        dkey = unpaired(dscores, q_rows).astype(BF16).astype(F32)
        cosine, sine = table[0], table[1]
        for i in range(PAIRS):
            part = dquery[LEN * i : LEN * i + LEN]
            dx_v[:, 128 * i : 128 * i + 128] = (part * cosine - partner(part) * sine).astype(BF16)
        dx_v[:, QW : QW + KV] = (dkey * cosine - partner(dkey) * sine).astype(BF16)
        dx_v[:, QW + KV :] = dvalue.astype(BF16)

        @pl.loop(0, CHUNKS)
        def _(i):
            wq_copy(i).wait()
            rows = pl.ds(pl.multiple_of(i * CHUNK, CHUNK), CHUNK)
            dn_v[:, rows] = dot_nt(dx_v[...], wq_v[rows, :]).astype(BF16)

        get_h.wait()
        wide = h_v[...].astype(F32)
        scale = inv_rms(wide)
        scaled = dn_v[...].astype(F32) * gain[...]
        inner = jnp.sum(scaled * wide, axis=1, keepdims=True)
        out[...] = (
            g_v[...].astype(F32)
            + scale * scaled
            - wide * (scale * scale * scale * inner * (1.0 / D))
        ).astype(BF16)
        put = pltpu.make_async_copy(out, grads.at[pl.ds(row0, LEN), :], sems.at[2])
        put.start()
        put.wait()


ANY = pl.BlockSpec(memory_space=pl.ANY)
VMEM = pl.BlockSpec(memory_space=pltpu.VMEM)
SMEM = pl.BlockSpec(memory_space=pltpu.SMEM)
LAYER_COST = pl.CostEstimate(
    flops=2 * LEN * D * (XW + QW), bytes_accessed=2 * D * (XW + QW), transcendentals=0
)
LIMIT = 40 * 1024 * 1024


def forward_layer(tick, last_stage, micro, meta, inbox, entry, gain, table, packed, w_out, state):
    return pl.pallas_call(
        functools.partial(forward_kernel, tick, last_stage, micro),
        out_shape=(
            jax.ShapeDtypeStruct((LEN, D), BF16),
            *(jax.ShapeDtypeStruct(a.shape, a.dtype) for a in state),
        ),
        in_specs=[SMEM, ANY, ANY, VMEM, VMEM, ANY, ANY, ANY, ANY, ANY],
        out_specs=(VMEM, ANY, ANY, ANY),
        input_output_aliases={7: 1, 8: 2, 9: 3},
        scratch_shapes=[
            pltpu.VMEM((D, XW), BF16),
            pltpu.VMEM((QW, D), BF16),
            pltpu.VMEM((LEN, D), BF16),
            pltpu.VMEM((LEN, D), BF16),
            pltpu.VMEM((LEN, XW), F32),
            pltpu.VMEM((LEN, XW), BF16),
            pltpu.VMEM((LEN, QW), BF16),
            pltpu.VMEM((8, D), F32),
            pltpu.SemaphoreType.DMA((CHUNKS,)),
            pltpu.SemaphoreType.DMA((CHUNKS,)),
            pltpu.SemaphoreType.DMA((4,)),
        ],
        compiler_params=pltpu.CompilerParams(vmem_limit_bytes=LIMIT),
        cost_estimate=LAYER_COST,
        name="forward_layer",
    )(meta, inbox, entry, gain, table, packed, w_out, *state)


def backward_layer(
    tick, last_stage, micro, meta, inbox, seed, gain, table, packed, w_out, stash, grads
):
    return pl.pallas_call(
        functools.partial(backward_kernel, tick, last_stage, micro),
        out_shape=(
            jax.ShapeDtypeStruct((LEN, D), BF16),
            jax.ShapeDtypeStruct(grads.shape, grads.dtype),
        ),
        in_specs=[SMEM, VMEM, VMEM, VMEM, VMEM, ANY, ANY, ANY, ANY, ANY],
        out_specs=(VMEM, ANY),
        input_output_aliases={9: 1},
        scratch_shapes=[
            pltpu.VMEM((D, XW), BF16),
            pltpu.VMEM((QW, D), BF16),
            pltpu.VMEM((LEN, D), BF16),
            pltpu.VMEM((LEN, D), BF16),
            pltpu.VMEM((LEN, XW), BF16),
            pltpu.VMEM((LEN, QW), F32),
            pltpu.VMEM((LEN, XW), BF16),
            pltpu.VMEM((LEN, D), BF16),
            pltpu.SemaphoreType.DMA((CHUNKS,)),
            pltpu.SemaphoreType.DMA((CHUNKS,)),
            pltpu.SemaphoreType.DMA((3,)),
        ],
        compiler_params=pltpu.CompilerParams(vmem_limit_bytes=LIMIT),
        cost_estimate=LAYER_COST,
        name="backward_layer",
    )(meta, inbox, seed, gain, table, packed, w_out, *stash, grads)


def embed_kernel(last, final_gain, labels, out):
    rows = jnp.concatenate([last[j, 0:1, :] for j in (0, 2, 1, 3)] + [jnp.zeros((4, D), F32)], axis=0)
    pooled = rows * inv_rms(rows) * final_gain[...]
    size = jnp.sum(pooled * pooled, axis=1, keepdims=True)
    row = lax.broadcasted_iota(jnp.int32, (8, D), 0)
    unit = jnp.where(row < 4, pooled * lax.rsqrt(jnp.where(size > 0.0, size, 1.0)), 0.0)
    which = lax.broadcasted_iota(jnp.int32, (8, 128), 0)
    label = jnp.where(which == 0, labels[0], jnp.where(which == 1, labels[1], 0)).astype(F32)
    out[:, :D] = unit.astype(BF16)
    out[:, D:] = label.astype(BF16)


def embed(last, final_gain, labels):
    return pl.pallas_call(
        embed_kernel,
        out_shape=jax.ShapeDtypeStruct((8, D + 128), BF16),
        in_specs=[VMEM, VMEM, SMEM],
        out_specs=VMEM,
        name="embed",
    )(last, final_gain, labels)


def loss_kernel(me, last, final_gain, everyone, seed):
    count = everyone.shape[0]
    emb = everyone[:, :D]
    label = everyone[:, D:].astype(F32)[:, 0:1].astype(jnp.int32)
    scores = dot_nt(emb, emb) * SHARP
    row = lax.broadcasted_iota(jnp.int32, (count, count), 0)
    col = lax.broadcasted_iota(jnp.int32, (count, count), 1)
    valid = jnp.logical_and(lax.rem(row, 4) < 2, lax.rem(col, 4) >= 2)
    weights = jnp.where(valid, jnp.exp(scores), 0.0)
    total = jnp.sum(weights, axis=1, keepdims=True)
    prob = weights / jnp.where(total > 0.0, total, 1.0)
    target = lax.div(label, 2) * 4 + 2 + lax.rem(label, 2)
    hit = jnp.logical_and(valid, col == target)
    coef = (prob - hit.astype(F32)) * (COEF * SHARP)
    coef = jnp.where(valid, coef, 0.0)
    both = coef + coef.T
    mine = lax.broadcasted_iota(jnp.int32, (8, count), 0)
    pick = lax.broadcasted_iota(jnp.int32, (8, count), 1) == me[0] * 4 + mine
    pick = jnp.logical_and(pick, mine < 4).astype(F32)
    own = lax.dot_general(
        pick, both, (((1,), (0,)), ((), ())), precision=lax.Precision.HIGHEST,
        preferred_element_type=F32,
    )
    top = own.astype(BF16)
    rest = own - top.astype(F32)
    mid = rest.astype(BF16)
    low = (rest - mid.astype(F32)).astype(BF16)
    grad = dot_nn(top, emb) + (dot_nn(mid, emb) + dot_nn(low, emb))
    rows = jnp.concatenate([last[j, 0:1, :] for j in (0, 2, 1, 3)] + [jnp.zeros((4, D), F32)], axis=0)
    gain = final_gain[...]
    scale = inv_rms(rows)
    pooled = rows * scale * gain
    size = jnp.sum(pooled * pooled, axis=1, keepdims=True)
    norm = lax.rsqrt(jnp.where(size > 0.0, size, 1.0))
    unit = pooled * norm
    dpooled = norm * (grad - unit * jnp.sum(grad * unit, axis=1, keepdims=True))
    scaled = dpooled * gain
    inner = jnp.sum(scaled * rows, axis=1, keepdims=True)
    drow = scale * scaled - rows * (scale * scale * scale * inner * (1.0 / D))
    drow = drow.astype(BF16).astype(F32)
    seed[...] = jnp.concatenate(
        [drow[0:1], drow[2:3], drow[1:2], drow[3:4], jnp.zeros((4, D), F32)], axis=0
    )


def loss_seed(me, last, final_gain, everyone):
    return pl.pallas_call(
        loss_kernel,
        out_shape=jax.ShapeDtypeStruct((8, D), F32),
        in_specs=[SMEM, VMEM, VMEM, VMEM],
        out_specs=VMEM,
        name="loss_seed",
    )(me, last, final_gain, everyone)


def rotary_table():
    lane = jnp.arange(128, dtype=jnp.int32)
    frequency = ROPE_BASE ** (-(lane % 32).astype(F32) * (2.0 / HEAD_DIM))
    angles = jnp.arange(LEN, dtype=F32)[:, None] * frequency[None, :]
    sign = jnp.where(lane % 64 < 32, -1.0, 1.0)
    return jnp.stack([jnp.cos(angles), jnp.sin(angles) * sign])


def per_device(entry, norm_gain, w_qkv, w_out, final_gain, lengths, positive):
    stage = lax.axis_index("section")
    stages = lax.axis_size("section")
    replica = lax.axis_index(DP)
    micro = lengths.shape[0]
    shard = jnp.concatenate([w_qkv[0], w_out[0].reshape(-1, QW)], axis=1)
    packed = lax.all_gather(shard, DP, axis=0, tiled=True)
    full_out = packed[:, XW:].reshape(QW, D)
    meta = jnp.concatenate([stage.reshape(1), lengths]).astype(jnp.int32)
    table = rotary_table()
    gain = norm_gain
    ticks = micro + stages - 1
    rows = micro * LEN
    state = (
        jnp.zeros((rows, D), BF16),
        jnp.zeros((rows, XW), BF16),
        jnp.zeros((micro, 8, D), F32),
    )
    inbox = entry[:LEN]
    for tick in range(ticks):
        out, *state = forward_layer(
            tick, stages - 1, micro, meta, inbox, entry, gain, table, packed, full_out, state
        )
        if tick < ticks - 1:
            pairs = [(s, s + 1) for s in range(stages - 1) if 0 <= tick - s < micro]
            inbox = lax.ppermute(out, "section", pairs)
    stash_h, stash_x, last = state
    final_row = final_gain[None, :]
    mine = embed(last, final_row, positive)[:4]
    count = lax.axis_size(DP)
    copies = jnp.broadcast_to(mine, (count, *mine.shape))
    everyone = lax.all_to_all(copies, DP, split_axis=0, concat_axis=0, tiled=True)
    everyone = everyone.reshape(count * 4, D + 128)
    seed = loss_seed(replica.reshape(1), last, final_row, everyone)
    grads = jnp.zeros((rows, D), BF16)
    for tick in range(ticks):
        out, grads = backward_layer(
            tick, stages - 1, micro, meta, inbox, seed, gain, table, packed, full_out,
            (stash_h, stash_x), grads,
        )
        if tick < ticks - 1:
            pairs = [
                (stages - 1 - s, stages - 2 - s)
                for s in range(stages - 1)
                if 0 <= tick - s < micro
            ]
            inbox = lax.ppermute(out, "section", pairs)
    return grads[None]


def solution(mesh):
    finer = Mesh(
        mesh.devices.reshape(mesh.shape["section"], 4, 4, 2), ("section", "dp_0", "dp_1", "dp_2")
    )
    in_specs = (
        P(DP, None),
        P("section", None),
        P("section", DP, None),
        P("section", DP, None),
        P(),
        P(DP),
        P(DP),
    )
    return jax.shard_map(
        per_device,
        mesh=finer,
        in_specs=in_specs,
        out_specs=P("section", DP, None),
        check_vma=False,
    )
```

time: 974 us -> 545 us (0.56)
  the two profiles are of different devices: /device:TPU:1 before, /device:TPU:2 now
where the time goes in v1:
time: 545 us; the launch traced here: 535 us
  waiting for transfers between devices  367 us (67%)
  Pallas kernels  87.2 us (16%)
  starting transfers between devices  33.6 us (6%)
  local copies, waits for them, and re-layouts  30.9 us (6%)
  between operations  14.2 us (3%)
    ppermute x20, waiting for transfers between devices, per_device(): inbox = lax.ppermute(out, 'section', pairs)  279 us
    all_gather x1, waiting for transfers between devices, per_device(): packed = lax.all_gather(shard, DP, axis=0, tiled=True)  75.1 us
    pallas_call x11, Pallas kernels, backward_layer(): pl.pallas_call(functools.partial(backward_kernel, tick, last_stage, micro...  45.7 us
    pallas_call x11, Pallas kernels, forward_layer(): pl.pallas_call(functools.partial(forward_kernel, tick, last_stage, micro)...  35.5 us
    ppermute x20, starting transfers between devices, per_device(): inbox = lax.ppermute(out, 'section', pairs)  27.9 us
    all_to_all x1, waiting for transfers between devices, per_device(): lax.all_to_all(copies, DP, split_axis=0, concat_axis=0, tiled=True)  13.5 us
  transfers between devices with their start and end apart: 22, of which 10 were waited for; matrix products, arithmetic and copies ran while one was open for 0% of the time, Pallas kernels for 0%

profile of v1, /device:TPU:2, one launch (start us, length us, event | category | flops | bytes accessed | tf_op | source)
XLA Modules:
  0.0 535.2 jit_solution(9601299246911347275)
XLA Ops:
  10.5 75.1 %all-gather.2.cloned.1.call-done.packed = bf16[3584,2048]{1,0:T(8,128)(2,1)} async-done(((bf16[112,2048]{1,0:T(8,128)(2,1)}), bf16[3584,2048]{1,0:T(8,128)(2,1)}) %all-gather.2.cloned.1.call-update) | async-done | bytes 14680080 | tf_op jit(solution)/shard_map/all_gather | solution.py:495
  85.6 6.1 %slice.12 = bf16[3584,896]{1,0:T(8,128)(2,1)} slice(bf16[3584,2048]{1,0:T(8,128)(2,1)} %all-gather.2.cloned.1.call-done.packed), slice={[0:3584], [1152:2048]} | slice | bytes 12845056 | tf_op jit(solution)/shard_map/slice | solution.py:496
  91.7 10.6 %reshape.121.w_out = bf16[896,3584]{1,0:T(8,128)(2,1)} reshape(bf16[3584,896]{1,0:T(8,128)(2,1)} %slice.12) | data formatting | bytes 12845056 | tf_op jit(solution)/shard_map/reshape | solution.py:496
  106.1 7.6 %forward_layer.11 = (bf16[48,3584]{1,0:T(8,128)(2,1)S(1)}, bf16[192,3584]{1,0:T(8,128)(2,1)S(1)}, bf16[192,1152]{1,0:T(8,128)(2,1)S(1)}, f32[4,8,3584]{2,1,0:T(8,128)S(1)}) custom-call(s32[5]{0:T(128)S(1)} %pad_add_fusion.meta, bf16[48,3584]{1,0:T(8,128)(2,1)S(1)} %copy-done.7, ...), custom_call_target="tpu_custom_call", output_to_operand_aliasing={{1}: (7, {}), {2}: (8, {}), {3}: (9, {})} | custom-call | flops 704643072 | bytes 14680064 | tf_op jit(solution)/shard_map/forward_layer/pallas_call | solution.py:345
  115.0 8.0 %collective-permute-done.inbox = bf16[48,3584]{1,0:T(8,128)(2,1)S(1)} collective-permute-done((bf16[48,3584]{1,0:T(8,128)(2,1)S(1)}, bf16[48,3584]{1,0:T(8,128)(2,1)S(1)}, u32[]{:S(2)}, u32[]{:S(2)}) %collective-permute-start) | collective-permute-done | bytes 344096 | tf_op jit(solution)/shard_map/ppermute | solution.py:514
  123.0 7.3 %forward_layer.12 = (bf16[48,3584]{1,0:T(8,128)(2,1)S(1)}, bf16[192,3584]{1,0:T(8,128)(2,1)S(1)}, bf16[192,1152]{1,0:T(8,128)(2,1)S(1)}, f32[4,8,3584]{2,1,0:T(8,128)S(1)}) custom-call(s32[5]{0:T(128)S(1)} %pad_add_fusion.meta, bf16[48,3584]{1,0:T(8,128)(2,1)S(1)} %collective-permute-done.inbox, ...), custom_call_target="tpu_custom_call", output_to_operand_aliasing={{1}: (7, {}), {2}: (8, {}), {3}: (9, {})} | custom-call | flops 704643072 | bytes 14680064 | tf_op jit(solution)/shard_map/forward_layer/pallas_call | solution.py:345
  130.3 4.4 collective-permute-start.1
  134.7 7.1 %collective-permute-done.1.inbox = bf16[48,3584]{1,0:T(8,128)(2,1)S(1)} collective-permute-done((bf16[48,3584]{1,0:T(8,128)(2,1)S(1)}, bf16[48,3584]{1,0:T(8,128)(2,1)S(1)}, u32[]{:S(2)}, u32[]{:S(2)}) %collective-permute-start.1) | collective-permute-done | bytes 344096 | tf_op jit(solution)/shard_map/ppermute | solution.py:514
  141.8 7.3 %forward_layer.13 = (bf16[48,3584]{1,0:T(8,128)(2,1)S(1)}, bf16[192,3584]{1,0:T(8,128)(2,1)S(1)}, bf16[192,1152]{1,0:T(8,128)(2,1)S(1)}, f32[4,8,3584]{2,1,0:T(8,128)S(1)}) custom-call(s32[5]{0:T(128)S(1)} %pad_add_fusion.meta, bf16[48,3584]{1,0:T(8,128)(2,1)S(1)} %collective-permute-done.1.inbox, ...), custom_call_target="tpu_custom_call", output_to_operand_aliasing={{1}: (7, {}), {2}: (8, {}), {3}: (9, {})} | custom-call | flops 704643072 | bytes 14680064 | tf_op jit(solution)/shard_map/forward_layer/pallas_call | solution.py:345
  149.1 4.4 collective-permute-start.2
  153.5 6.3 %collective-permute-done.2.inbox = bf16[48,3584]{1,0:T(8,128)(2,1)S(1)} collective-permute-done((bf16[48,3584]{1,0:T(8,128)(2,1)S(1)}, bf16[48,3584]{1,0:T(8,128)(2,1)S(1)}, u32[]{:S(2)}, u32[]{:S(2)}) %collective-permute-start.2) | collective-permute-done | bytes 344096 | tf_op jit(solution)/shard_map/ppermute | solution.py:514
  159.8 7.3 %forward_layer.14 = (bf16[48,3584]{1,0:T(8,128)(2,1)S(1)}, bf16[192,3584]{1,0:T(8,128)(2,1)S(1)}, bf16[192,1152]{1,0:T(8,128)(2,1)S(1)}, f32[4,8,3584]{2,1,0:T(8,128)S(1)}) custom-call(s32[5]{0:T(128)S(1)} %pad_add_fusion.meta, bf16[48,3584]{1,0:T(8,128)(2,1)S(1)} %collective-permute-done.2.inbox, ...), custom_call_target="tpu_custom_call", output_to_operand_aliasing={{1}: (7, {}), {2}: (8, {}), {3}: (9, {})} | custom-call | flops 704643072 | bytes 14680064 | tf_op jit(solution)/shard_map/forward_layer/pallas_call | solution.py:345
  167.1 4.4 collective-permute-start.3
  171.5 5.4 %collective-permute-done.3.inbox = bf16[48,3584]{1,0:T(8,128)(2,1)S(1)} collective-permute-done((bf16[48,3584]{1,0:T(8,128)(2,1)S(1)}, bf16[48,3584]{1,0:T(8,128)(2,1)S(1)}, u32[]{:S(2)}, u32[]{:S(2)}) %collective-permute-start.3) | collective-permute-done | bytes 344096 | tf_op jit(solution)/shard_map/ppermute | solution.py:514
  192.6 5.7 %all-to-all-start = ((bf16[32,4,3712]{2,1,0:T(4,128)(2,1)}), bf16[32,4,3712]{2,1,0:T(4,128)(2,1)S(1)}, u32[]{:S(2)}, u32[]{:S(2)}) async-start(bf16[32,4,3712]{2,1,0:T(4,128)(2,1)} %broadcast_in_dim.31), calls=%async_computation | async-start | bytes 1900544 | tf_op jit(solution)/shard_map/all_to_all | solution.py:520
  198.3 13.5 %all-to-all-done = bf16[32,4,3712]{2,1,0:T(4,128)(2,1)S(1)} async-done(((bf16[32,4,3712]{2,1,0:T(4,128)(2,1)}), bf16[32,4,3712]{2,1,0:T(4,128)(2,1)S(1)}, u32[]{:S(2)}, u32[]{:S(2)}) %all-to-all-start) | async-done | bytes 950304 | tf_op jit(solution)/shard_map/all_to_all | solution.py:520
  231.7 227.0 %collective-permute-done.16.inbox = bf16[48,3584]{1,0:T(8,128)(2,1)S(1)} collective-permute-done((bf16[48,3584]{1,0:T(8,128)(2,1)S(1)}, bf16[48,3584]{1,0:T(8,128)(2,1)S(1)}, u32[]{:S(2)}, u32[]{:S(2)}) %collective-permute-start.16) | collective-permute-done | bytes 344096 | tf_op jit(solution)/shard_map/ppermute | solution.py:535
  458.7 9.9 %backward_layer.18 = (bf16[48,3584]{1,0:T(8,128)(2,1)S(1)}, bf16[192,3584]{1,0:T(8,128)(2,1)}) custom-call(s32[5]{0:T(128)S(1)} %pad_add_fusion.meta, bf16[48,3584]{1,0:T(8,128)(2,1)S(1)} %collective-permute-done.16.inbox, f32[8,3584]{1,0:T(8,128)S(1)} %copy-done.5, f32[1,3584]{1,0:T(1,128)S(1)} %copy-done.6, ...), custom_call_target="tpu_custom_call", output_to_operand_aliasing={{1}: (9, {})} | custom-call | flops 704643072 | bytes 14680064 | tf_op jit(solution)/shard_map/backward_layer/pallas_call | solution.py:376
  469.9 8.3 %collective-permute-done.17.inbox = bf16[48,3584]{1,0:T(8,128)(2,1)S(1)} collective-permute-done((bf16[48,3584]{1,0:T(8,128)(2,1)S(1)}, bf16[48,3584]{1,0:T(8,128)(2,1)S(1)}, u32[]{:S(2)}, u32[]{:S(2)}) %collective-permute-start.17) | collective-permute-done | bytes 344096 | tf_op jit(solution)/shard_map/ppermute | solution.py:535
  478.2 10.1 %backward_layer.19 = (bf16[48,3584]{1,0:T(8,128)(2,1)S(1)}, bf16[192,3584]{1,0:T(8,128)(2,1)}) custom-call(s32[5]{0:T(128)S(1)} %pad_add_fusion.meta, bf16[48,3584]{1,0:T(8,128)(2,1)S(1)} %collective-permute-done.17.inbox, f32[8,3584]{1,0:T(8,128)S(1)} %copy-done.5, f32[1,3584]{1,0:T(1,128)S(1)} %copy-done.6, ...), custom_call_target="tpu_custom_call", output_to_operand_aliasing={{1}: (9, {})} | custom-call | flops 704643072 | bytes 14680064 | tf_op jit(solution)/shard_map/backward_layer/pallas_call | solution.py:376
  489.6 8.8 %collective-permute-done.18.inbox = bf16[48,3584]{1,0:T(8,128)(2,1)S(1)} collective-permute-done((bf16[48,3584]{1,0:T(8,128)(2,1)S(1)}, bf16[48,3584]{1,0:T(8,128)(2,1)S(1)}, u32[]{:S(2)}, u32[]{:S(2)}) %collective-permute-start.18) | collective-permute-done | bytes 344096 | tf_op jit(solution)/shard_map/ppermute | solution.py:535
  498.4 9.9 %backward_layer.20 = (bf16[48,3584]{1,0:T(8,128)(2,1)S(1)}, bf16[192,3584]{1,0:T(8,128)(2,1)}) custom-call(s32[5]{0:T(128)S(1)} %pad_add_fusion.meta, bf16[48,3584]{1,0:T(8,128)(2,1)S(1)} %collective-permute-done.18.inbox, f32[8,3584]{1,0:T(8,128)S(1)} %copy-done.5, f32[1,3584]{1,0:T(1,128)S(1)} %copy-done.6, ...), custom_call_target="tpu_custom_call", output_to_operand_aliasing={{1}: (9, {})} | custom-call | flops 704643072 | bytes 14680064 | tf_op jit(solution)/shard_map/backward_layer/pallas_call | solution.py:376
  509.6 7.8 %collective-permute-done.19.inbox = bf16[48,3584]{1,0:T(8,128)(2,1)S(1)} collective-permute-done((bf16[48,3584]{1,0:T(8,128)(2,1)S(1)}, bf16[48,3584]{1,0:T(8,128)(2,1)S(1)}, u32[]{:S(2)}, u32[]{:S(2)}) %collective-permute-start.19) | collective-permute-done | bytes 344096 | tf_op jit(solution)/shard_map/ppermute | solution.py:535
  517.5 10.7 %backward_layer.21 = (bf16[48,3584]{1,0:T(8,128)(2,1)}, bf16[192,3584]{1,0:T(8,128)(2,1)}) custom-call(s32[5]{0:T(128)S(1)} %pad_add_fusion.meta, bf16[48,3584]{1,0:T(8,128)(2,1)S(1)} %collective-permute-done.19.inbox, f32[8,3584]{1,0:T(8,128)S(1)} %copy-done.5, f32[1,3584]{1,0:T(1,128)S(1)} %copy-done.6, ...), custom_call_target="tpu_custom_call", output_to_operand_aliasing={{1}: (9, {})} | custom-call | flops 704643072 | bytes 14680064 | tf_op jit(solution)/shard_map/backward_layer/pallas_call | solution.py:376
  (86 shorter events, 48.1 us)
Async XLA Ops:
  6.5 79.1 %all-gather.2.cloned.1.call-start = ((), (), s32[]{:S(2)}) async-start(), calls=%async_computation.1 | async-start | bytes 15138816 | tf_op jit(solution)/shard_map/all_gather | solution.py:495
  106.1 16.9 %copy-start.1 = (bf16[896,3584]{1,0:T(8,128)(2,1)S(1)}, bf16[896,3584]{1,0:T(8,128)(2,1)}, u32[]{:S(2)}) copy-start(bf16[896,3584]{1,0:T(8,128)(2,1)} %reshape.121.w_out) | copy-start | bytes 19267588
  113.7 9.3 %collective-permute-start = (bf16[48,3584]{1,0:T(8,128)(2,1)S(1)}, bf16[48,3584]{1,0:T(8,128)(2,1)S(1)}, u32[]{:S(2)}, u32[]{:S(2)}) collective-permute-start(bf16[48,3584]{1,0:T(8,128)(2,1)S(1)} %get-tuple-element.69), channel_id=1, source_target_pairs={{0,32},{1,33},{2,34},{3,35},{4,36},{5,37},{6,38},{7,39},{8,40},{9,... | collective-permute-start | bytes 1032200 | tf_op jit(solution)/shard_map/ppermute | solution.py:514
  130.3 11.5 %collective-permute-start.1 = (bf16[48,3584]{1,0:T(8,128)(2,1)S(1)}, bf16[48,3584]{1,0:T(8,128)(2,1)S(1)}, u32[]{:S(2)}, u32[]{:S(2)}) collective-permute-start(bf16[48,3584]{1,0:T(8,128)(2,1)S(1)} %get-tuple-element.73), channel_id=1, source_target_pairs={{0,32},{32,64},{1,33},{33,65},{2,34},{34,66},{3,35},{35,67},{4,36}... | collective-permute-start | bytes 1032200 | tf_op jit(solution)/shard_map/ppermute | solution.py:514
  149.1 10.7 %collective-permute-start.2 = (bf16[48,3584]{1,0:T(8,128)(2,1)S(1)}, bf16[48,3584]{1,0:T(8,128)(2,1)S(1)}, u32[]{:S(2)}, u32[]{:S(2)}) collective-permute-start(bf16[48,3584]{1,0:T(8,128)(2,1)S(1)} %get-tuple-element.77), channel_id=1, source_target_pairs={{0,32},{32,64},{64,96},{1,33},{33,65},{65,97},{2,34},{34,66},{66,9... | collective-permute-start | bytes 1032200 | tf_op jit(solution)/shard_map/ppermute | solution.py:514
  167.1 9.8 %collective-permute-start.3 = (bf16[48,3584]{1,0:T(8,128)(2,1)S(1)}, bf16[48,3584]{1,0:T(8,128)(2,1)S(1)}, u32[]{:S(2)}, u32[]{:S(2)}) collective-permute-start(bf16[48,3584]{1,0:T(8,128)(2,1)S(1)} %get-tuple-element.81), channel_id=1, source_target_pairs={{0,32},{32,64},{64,96},{96,128},{1,33},{33,65},{65,97},{97,129},{2... | collective-permute-start | bytes 1032200 | tf_op jit(solution)/shard_map/ppermute | solution.py:514
  177.6 0.7 collective-permute-start.4
  179.0 0.7 collective-permute-start.5
  180.5 0.7 collective-permute-start.6
  182.2 0.7 collective-permute-start.7
  183.7 0.7 collective-permute-start.8
  185.1 1.3 collective-permute-start.9
  192.6 19.3 %all-to-all-start = ((bf16[32,4,3712]{2,1,0:T(4,128)(2,1)}), bf16[32,4,3712]{2,1,0:T(4,128)(2,1)S(1)}, u32[]{:S(2)}, u32[]{:S(2)}) async-start(bf16[32,4,3712]{2,1,0:T(4,128)(2,1)} %broadcast_in_dim.31), calls=%async_computation | async-start | bytes 1900544 | tf_op jit(solution)/shard_map/all_to_all | solution.py:520
  213.0 5.2 copy-start.9
  221.7 0.7 collective-permute-start.10
  223.1 0.7 collective-permute-start.11
  224.7 0.7 collective-permute-start.12
  226.1 0.7 collective-permute-start.13
  227.6 0.7 collective-permute-start.14
  229.0 0.7 collective-permute-start.15
  230.4 228.3 %collective-permute-start.16 = (bf16[48,3584]{1,0:T(8,128)(2,1)S(1)}, bf16[48,3584]{1,0:T(8,128)(2,1)S(1)}, u32[]{:S(2)}, u32[]{:S(2)}) collective-permute-start(bf16[48,3584]{1,0:T(8,128)(2,1)S(1)} %get-tuple-element.124), channel_id=1, source_target_pairs={{128,96},{96,64},{64,32},{32,0},{129,97},{97,65},{65,33},{33,1},{1... | collective-permute-start | bytes 1032200 | tf_op jit(solution)/shard_map/ppermute | solution.py:535
  468.6 9.6 %collective-permute-start.17 = (bf16[48,3584]{1,0:T(8,128)(2,1)S(1)}, bf16[48,3584]{1,0:T(8,128)(2,1)S(1)}, u32[]{:S(2)}, u32[]{:S(2)}) collective-permute-start(bf16[48,3584]{1,0:T(8,128)(2,1)S(1)} %get-tuple-element.126), channel_id=1, source_target_pairs={{96,64},{64,32},{32,0},{97,65},{65,33},{33,1},{98,66},{66,34},{34,... | collective-permute-start | bytes 1032200 | tf_op jit(solution)/shard_map/ppermute | solution.py:535
  488.3 10.1 %collective-permute-start.18 = (bf16[48,3584]{1,0:T(8,128)(2,1)S(1)}, bf16[48,3584]{1,0:T(8,128)(2,1)S(1)}, u32[]{:S(2)}, u32[]{:S(2)}) collective-permute-start(bf16[48,3584]{1,0:T(8,128)(2,1)S(1)} %get-tuple-element.128), channel_id=1, source_target_pairs={{64,32},{32,0},{65,33},{33,1},{66,34},{34,2},{67,35},{35,3},{68,36... | collective-permute-start | bytes 1032200 | tf_op jit(solution)/shard_map/ppermute | solution.py:535
  508.3 9.1 %collective-permute-start.19 = (bf16[48,3584]{1,0:T(8,128)(2,1)S(1)}, bf16[48,3584]{1,0:T(8,128)(2,1)S(1)}, u32[]{:S(2)}, u32[]{:S(2)}) collective-permute-start(bf16[48,3584]{1,0:T(8,128)(2,1)S(1)} %get-tuple-element.130), channel_id=1, source_target_pairs={{32,0},{33,1},{34,2},{35,3},{36,4},{37,5},{38,6},{39,7},{40,8},{41... | collective-permute-start | bytes 1032200 | tf_op jit(solution)/shard_map/ppermute | solution.py:535
  (10 other events, 18.9 us)
Sparse Core Ops, SparseCore 0:
  9.9 75.6 all-gather.1

commit v2 on v1

--- a/solution.py
+++ b/solution.py
@@ -23,6 +23,7 @@
 COEF = 256.0
 CHUNK = 512
 CHUNKS = D // CHUNK
+STAGGER = 4200
 F32 = jnp.float32
 BF16 = jnp.bfloat16
 
@@ -114,8 +115,8 @@
     entry,
     gain,
     table,
-    packed,
-    w_out,
+    wq,
+    wo,
     stash_h_in,
     stash_x_in,
     last_in,
@@ -123,16 +124,12 @@
     stash_h,
     stash_x,
     last,
-    wq_v,
-    wo_v,
     h_v,
     n_v,
     acc_v,
     x_v,
     ctx_v,
     last_v,
-    wq_sem,
-    wo_sem,
     sems,
 ):
     del stash_h_in, stash_x_in, last_in
@@ -144,16 +141,6 @@
         length = meta[1 + slot]
         row0 = pl.multiple_of(slot * LEN, LEN)
 
-        def wq_copy(i):
-            rows = pl.ds(pl.multiple_of(i * CHUNK, CHUNK), CHUNK)
-            return pltpu.make_async_copy(
-                packed.at[rows, pl.ds(0, XW)], wq_v.at[rows, :], wq_sem.at[i]
-            )
-
-        def wo_copy(i):
-            cols = pl.ds(pl.multiple_of(i * CHUNK, CHUNK), CHUNK)
-            return pltpu.make_async_copy(w_out.at[:, cols], wo_v.at[:, cols], wo_sem.at[i])
-
         first = pltpu.make_async_copy(entry.at[pl.ds(row0, LEN), :], h_v, sems.at[0])
         later = pltpu.make_async_copy(inbox, h_v, sems.at[0])
 
@@ -165,10 +152,12 @@
         def _():
             later.start()
 
-        for i in range(CHUNKS):
-            wq_copy(i).start()
-        for i in range(CHUNKS):
-            wo_copy(i).start()
+        if tick == 0:
+
+            @pl.when(meta[1 + micro] == 1)
+            def _():
+                pl.delay(STAGGER)
+
         later.wait()
         keep_h = pltpu.make_async_copy(h_v, stash_h.at[pl.ds(row0, LEN), :], sems.at[1])
         keep_h.start()
@@ -178,9 +167,8 @@
 
         @pl.loop(0, CHUNKS)
         def _(i):
-            wq_copy(i).wait()
             cols = pl.ds(pl.multiple_of(i * CHUNK, CHUNK), CHUNK)
-            acc_v[...] += dot_nn(n_v[:, cols], wq_v[cols, :])
+            acc_v[...] += dot_nn(n_v[:, cols], wq[cols, :])
 
         cosine, sine = table[0], table[1]
         for i in range(PAIRS + 1):
@@ -198,9 +186,8 @@
 
         @pl.loop(0, CHUNKS)
         def _(i):
-            wo_copy(i).wait()
             cols = pl.ds(pl.multiple_of(i * CHUNK, CHUNK), CHUNK)
-            branch = dot_nn(ctx_v[...], wo_v[:, cols])
+            branch = dot_nn(ctx_v[...], wo[:, cols])
             out[:, cols] = (h_v[:, cols].astype(F32) + branch).astype(BF16)
 
         @pl.when(stage == last_stage)
@@ -225,23 +212,19 @@
     seed,
     gain,
     table,
-    packed,
-    w_out,
+    wq,
+    wo,
     stash_h,
     stash_x,
     grads_in,
     out,
     grads,
-    wq_v,
-    wo_v,
     h_v,
     g_v,
     x_v,
     dctx_v,
     dx_v,
     dn_v,
-    wq_sem,
-    wo_sem,
     sems,
 ):
     del grads_in
@@ -253,24 +236,16 @@
         length = meta[1 + slot]
         row0 = pl.multiple_of(slot * LEN, LEN)
 
-        def wq_copy(i):
-            rows = pl.ds(pl.multiple_of(i * CHUNK, CHUNK), CHUNK)
-            return pltpu.make_async_copy(
-                packed.at[rows, pl.ds(0, XW)], wq_v.at[rows, :], wq_sem.at[i]
-            )
-
-        def wo_copy(i):
-            cols = pl.ds(pl.multiple_of(i * CHUNK, CHUNK), CHUNK)
-            return pltpu.make_async_copy(w_out.at[:, cols], wo_v.at[:, cols], wo_sem.at[i])
-
-        for i in range(CHUNKS):
-            wo_copy(i).start()
         get_x = pltpu.make_async_copy(stash_x.at[pl.ds(row0, LEN), :], x_v, sems.at[0])
         get_h = pltpu.make_async_copy(stash_h.at[pl.ds(row0, LEN), :], h_v, sems.at[1])
         get_x.start()
         get_h.start()
-        for i in range(CHUNKS):
-            wq_copy(i).start()
+        if tick == 0:
+
+            @pl.when(meta[1 + micro] == 1)
+            def _():
+                pl.delay(STAGGER)
+
 
         @pl.when(stage == last_stage)
         def _():
@@ -287,9 +262,8 @@
 
         @pl.loop(0, CHUNKS)
         def _(i):
-            wo_copy(i).wait()
             cols = pl.ds(pl.multiple_of(i * CHUNK, CHUNK), CHUNK)
-            dctx_v[...] += dot_nt(g_v[:, cols], wo_v[:, cols])
+            dctx_v[...] += dot_nt(g_v[:, cols], wo[:, cols])
 
         get_x.wait()
         q_rows = rows_of(x_v)
@@ -313,9 +287,8 @@
 
         @pl.loop(0, CHUNKS)
         def _(i):
-            wq_copy(i).wait()
             rows = pl.ds(pl.multiple_of(i * CHUNK, CHUNK), CHUNK)
-            dn_v[:, rows] = dot_nt(dx_v[...], wq_v[rows, :]).astype(BF16)
+            dn_v[:, rows] = dot_nt(dx_v[...], wq[rows, :]).astype(BF16)
 
         get_h.wait()
         wide = h_v[...].astype(F32)
@@ -338,40 +311,37 @@
 LAYER_COST = pl.CostEstimate(
     flops=2 * LEN * D * (XW + QW), bytes_accessed=2 * D * (XW + QW), transcendentals=0
 )
-LIMIT = 40 * 1024 * 1024
-
-
-def forward_layer(tick, last_stage, micro, meta, inbox, entry, gain, table, packed, w_out, state):
+LIMIT = 24 * 1024 * 1024
+SMALL = 8 * 1024 * 1024
+
+
+def forward_layer(tick, last_stage, micro, meta, inbox, entry, gain, table, wq, wo, state):
     return pl.pallas_call(
         functools.partial(forward_kernel, tick, last_stage, micro),
         out_shape=(
             jax.ShapeDtypeStruct((LEN, D), BF16),
             *(jax.ShapeDtypeStruct(a.shape, a.dtype) for a in state),
         ),
-        in_specs=[SMEM, ANY, ANY, VMEM, VMEM, ANY, ANY, ANY, ANY, ANY],
+        in_specs=[SMEM, ANY, ANY, VMEM, VMEM, VMEM, VMEM, ANY, ANY, ANY],
         out_specs=(VMEM, ANY, ANY, ANY),
         input_output_aliases={7: 1, 8: 2, 9: 3},
         scratch_shapes=[
-            pltpu.VMEM((D, XW), BF16),
-            pltpu.VMEM((QW, D), BF16),
             pltpu.VMEM((LEN, D), BF16),
             pltpu.VMEM((LEN, D), BF16),
             pltpu.VMEM((LEN, XW), F32),
             pltpu.VMEM((LEN, XW), BF16),
             pltpu.VMEM((LEN, QW), BF16),
             pltpu.VMEM((8, D), F32),
-            pltpu.SemaphoreType.DMA((CHUNKS,)),
-            pltpu.SemaphoreType.DMA((CHUNKS,)),
             pltpu.SemaphoreType.DMA((4,)),
         ],
         compiler_params=pltpu.CompilerParams(vmem_limit_bytes=LIMIT),
         cost_estimate=LAYER_COST,
         name="forward_layer",
-    )(meta, inbox, entry, gain, table, packed, w_out, *state)
+    )(meta, inbox, entry, gain, table, wq, wo, *state)
 
 
 def backward_layer(
-    tick, last_stage, micro, meta, inbox, seed, gain, table, packed, w_out, stash, grads
+    tick, last_stage, micro, meta, inbox, seed, gain, table, wq, wo, stash, grads
 ):
     return pl.pallas_call(
         functools.partial(backward_kernel, tick, last_stage, micro),
@@ -379,84 +349,152 @@
             jax.ShapeDtypeStruct((LEN, D), BF16),
             jax.ShapeDtypeStruct(grads.shape, grads.dtype),
         ),
-        in_specs=[SMEM, VMEM, VMEM, VMEM, VMEM, ANY, ANY, ANY, ANY, ANY],
+        in_specs=[SMEM, VMEM, VMEM, VMEM, VMEM, VMEM, VMEM, ANY, ANY, ANY],
         out_specs=(VMEM, ANY),
         input_output_aliases={9: 1},
         scratch_shapes=[
-            pltpu.VMEM((D, XW), BF16),
-            pltpu.VMEM((QW, D), BF16),
             pltpu.VMEM((LEN, D), BF16),
             pltpu.VMEM((LEN, D), BF16),
             pltpu.VMEM((LEN, XW), BF16),
             pltpu.VMEM((LEN, QW), F32),
             pltpu.VMEM((LEN, XW), BF16),
             pltpu.VMEM((LEN, D), BF16),
-            pltpu.SemaphoreType.DMA((CHUNKS,)),
-            pltpu.SemaphoreType.DMA((CHUNKS,)),
             pltpu.SemaphoreType.DMA((3,)),
         ],
         compiler_params=pltpu.CompilerParams(vmem_limit_bytes=LIMIT),
         cost_estimate=LAYER_COST,
         name="backward_layer",
-    )(meta, inbox, seed, gain, table, packed, w_out, *stash, grads)
+    )(meta, inbox, seed, gain, table, wq, wo, *stash, grads)
+
+
+def pack_kernel(w_qkv, w_out, shard):
+    shard[:, :XW] = w_qkv[...]
+    pieces = [w_out[:, QW * j : QW * j + QW].astype(F32) for j in range(D // QW)]
+    shard[:, XW:] = jnp.concatenate(pieces, axis=0).astype(BF16)
+
+
+def pack(w_qkv, w_out):
+    return pl.pallas_call(
+        pack_kernel,
+        out_shape=jax.ShapeDtypeStruct((w_qkv.shape[0], PACK), BF16),
+        in_specs=[VMEM, VMEM],
+        out_specs=VMEM,
+        compiler_params=pltpu.CompilerParams(vmem_limit_bytes=SMALL),
+        name="pack",
+    )(w_qkv, w_out)
+
+
+def unpack_kernel(packed, wq, wo, part_v, sems):
+    parts = D // QW
+    groups = 8
+    rows = D // groups
+    short = rows // (4 * parts)
+    whole = pltpu.make_async_copy(packed.at[:, pl.ds(0, XW)], wq, sems.at[groups])
+
+    def piece(i):
+        at = pl.ds(pl.multiple_of(i * rows, rows), rows)
+        return pltpu.make_async_copy(packed.at[at, pl.ds(XW, QW)], part_v.at[at, :], sems.at[i])
+
+    for i in range(groups):
+        piece(i).start()
+    whole.start()
+
+    @pl.loop(0, groups)
+    def _(i):
+        piece(i).wait()
+        blocks = []
+        for r in range(4):
+            at = pl.ds(pl.multiple_of(i * rows + r * (rows // 4), 16), rows // 4)
+            blocks.append(part_v[at, :].astype(F32))
+        to = pl.ds(pl.multiple_of(i * (rows // 4), 16), rows // 4)
+        for j in range(parts):
+            cut = [block[short * j : short * j + short] for block in blocks]
+            wo[to, QW * j : QW * j + QW] = jnp.concatenate(cut, axis=0).astype(BF16)
+
+    whole.wait()
+
+
+def unpack(packed):
+    return pl.pallas_call(
+        unpack_kernel,
+        out_shape=(jax.ShapeDtypeStruct((D, XW), BF16), jax.ShapeDtypeStruct((QW, D), BF16)),
+        in_specs=[ANY],
+        out_specs=(VMEM, VMEM),
+        scratch_shapes=[pltpu.VMEM((D, QW), BF16), pltpu.SemaphoreType.DMA((9,))],
+        compiler_params=pltpu.CompilerParams(vmem_limit_bytes=LIMIT),
+        name="unpack",
+    )(packed)
+
+
+HALF = D // 2
+WIDE = HALF + 128
+
+
+def pooled_rows(last):
+    return jnp.concatenate([last[j, 0:1, :] for j in (0, 2, 1, 3)], axis=0)
 
 
 def embed_kernel(last, final_gain, labels, out):
-    rows = jnp.concatenate([last[j, 0:1, :] for j in (0, 2, 1, 3)] + [jnp.zeros((4, D), F32)], axis=0)
+    rows = pooled_rows(last)
     pooled = rows * inv_rms(rows) * final_gain[...]
-    size = jnp.sum(pooled * pooled, axis=1, keepdims=True)
-    row = lax.broadcasted_iota(jnp.int32, (8, D), 0)
-    unit = jnp.where(row < 4, pooled * lax.rsqrt(jnp.where(size > 0.0, size, 1.0)), 0.0)
+    unit = pooled * lax.rsqrt(jnp.sum(pooled * pooled, axis=1, keepdims=True))
+    halves = jnp.concatenate([unit[:, :HALF], unit[:, HALF:]], axis=0).astype(BF16)
     which = lax.broadcasted_iota(jnp.int32, (8, 128), 0)
-    label = jnp.where(which == 0, labels[0], jnp.where(which == 1, labels[1], 0)).astype(F32)
-    out[:, :D] = unit.astype(BF16)
-    out[:, D:] = label.astype(BF16)
-
-
-def embed(last, final_gain, labels):
+    label = jnp.where(which == 0, labels[0], jnp.where(which == 1, labels[1], 0))
+    label = label.astype(F32).astype(BF16)
+    for i in range(out.shape[0]):
+        out[i, :, :HALF] = halves
+        out[i, :, HALF:] = label
+
+
+def embed(count, last, final_gain, labels):
     return pl.pallas_call(
-        embed_kernel,
-        out_shape=jax.ShapeDtypeStruct((8, D + 128), BF16),
+        functools.partial(embed_kernel),
+        out_shape=jax.ShapeDtypeStruct((count, 8, WIDE), BF16),
         in_specs=[VMEM, VMEM, SMEM],
         out_specs=VMEM,
+        compiler_params=pltpu.CompilerParams(vmem_limit_bytes=SMALL),
         name="embed",
     )(last, final_gain, labels)
 
 
 def loss_kernel(me, last, final_gain, everyone, seed):
     count = everyone.shape[0]
-    emb = everyone[:, :D]
-    label = everyone[:, D:].astype(F32)[:, 0:1].astype(jnp.int32)
-    scores = dot_nt(emb, emb) * SHARP
-    row = lax.broadcasted_iota(jnp.int32, (count, count), 0)
+    emb = everyone[:, :HALF]
+    label = everyone[:, HALF:].astype(F32)[:, 0:1].astype(jnp.int32)
+    scores = dot_nt(emb, emb)
+    scores = scores + pltpu.roll(pltpu.roll(scores, count - 4, 0), count - 4, 1)
+    row = lax.rem(lax.broadcasted_iota(jnp.int32, (count, count), 0), 8)
     col = lax.broadcasted_iota(jnp.int32, (count, count), 1)
-    valid = jnp.logical_and(lax.rem(row, 4) < 2, lax.rem(col, 4) >= 2)
-    weights = jnp.where(valid, jnp.exp(scores), 0.0)
+    doc = jnp.logical_and(lax.rem(col, 8) >= 2, lax.rem(col, 8) < 4)
+    valid = jnp.logical_and(row < 2, doc)
+    weights = jnp.where(valid, jnp.exp(scores * SHARP), 0.0)
     total = jnp.sum(weights, axis=1, keepdims=True)
-    prob = weights / jnp.where(total > 0.0, total, 1.0)
-    target = lax.div(label, 2) * 4 + 2 + lax.rem(label, 2)
-    hit = jnp.logical_and(valid, col == target)
-    coef = (prob - hit.astype(F32)) * (COEF * SHARP)
-    coef = jnp.where(valid, coef, 0.0)
+    prob = weights / jnp.where(row[:, :1] < 2, total, 1.0)
+    target = lax.div(label, 2) * 8 + 2 + lax.rem(label, 2)
+    coef = jnp.where(valid, (prob - (col == target).astype(F32)) * (COEF * SHARP), 0.0)
     both = coef + coef.T
     mine = lax.broadcasted_iota(jnp.int32, (8, count), 0)
-    pick = lax.broadcasted_iota(jnp.int32, (8, count), 1) == me[0] * 4 + mine
-    pick = jnp.logical_and(pick, mine < 4).astype(F32)
+    pick = lax.broadcasted_iota(jnp.int32, (8, count), 1) == me[0] * 8 + mine
     own = lax.dot_general(
-        pick, both, (((1,), (0,)), ((), ())), precision=lax.Precision.HIGHEST,
+        pick.astype(F32),
+        both,
+        (((1,), (0,)), ((), ())),
+        precision=lax.Precision.HIGHEST,
         preferred_element_type=F32,
-    )
+    )[:4]
+    own = jnp.concatenate([own, pltpu.roll(own, 4, 1)], axis=0)
     top = own.astype(BF16)
     rest = own - top.astype(F32)
     mid = rest.astype(BF16)
     low = (rest - mid.astype(F32)).astype(BF16)
     grad = dot_nn(top, emb) + (dot_nn(mid, emb) + dot_nn(low, emb))
-    rows = jnp.concatenate([last[j, 0:1, :] for j in (0, 2, 1, 3)] + [jnp.zeros((4, D), F32)], axis=0)
+    grad = jnp.concatenate([grad[:4], grad[4:]], axis=1)
+    rows = pooled_rows(last)
     gain = final_gain[...]
     scale = inv_rms(rows)
     pooled = rows * scale * gain
-    size = jnp.sum(pooled * pooled, axis=1, keepdims=True)
-    norm = lax.rsqrt(jnp.where(size > 0.0, size, 1.0))
+    norm = lax.rsqrt(jnp.sum(pooled * pooled, axis=1, keepdims=True))
     unit = pooled * norm
     dpooled = norm * (grad - unit * jnp.sum(grad * unit, axis=1, keepdims=True))
     scaled = dpooled * gain
@@ -474,6 +512,7 @@
         out_shape=jax.ShapeDtypeStruct((8, D), F32),
         in_specs=[SMEM, VMEM, VMEM, VMEM],
         out_specs=VMEM,
+        compiler_params=pltpu.CompilerParams(vmem_limit_bytes=SMALL),
         name="loss_seed",
     )(me, last, final_gain, everyone)
 
@@ -491,10 +530,9 @@
     stages = lax.axis_size("section")
     replica = lax.axis_index(DP)
     micro = lengths.shape[0]
-    shard = jnp.concatenate([w_qkv[0], w_out[0].reshape(-1, QW)], axis=1)
-    packed = lax.all_gather(shard, DP, axis=0, tiled=True)
-    full_out = packed[:, XW:].reshape(QW, D)
-    meta = jnp.concatenate([stage.reshape(1), lengths]).astype(jnp.int32)
+    core = lax.axis_index("dp_2")
+    wq, wo = unpack(lax.all_gather(pack(w_qkv[0], w_out[0]), DP, axis=0, tiled=True))
+    meta = jnp.concatenate([stage.reshape(1), lengths, core.reshape(1)]).astype(jnp.int32)
     table = rotary_table()
     gain = norm_gain
     ticks = micro + stages - 1
@@ -507,23 +545,22 @@
     inbox = entry[:LEN]
     for tick in range(ticks):
         out, *state = forward_layer(
-            tick, stages - 1, micro, meta, inbox, entry, gain, table, packed, full_out, state
+            tick, stages - 1, micro, meta, inbox, entry, gain, table, wq, wo, state
         )
         if tick < ticks - 1:
             pairs = [(s, s + 1) for s in range(stages - 1) if 0 <= tick - s < micro]
             inbox = lax.ppermute(out, "section", pairs)
     stash_h, stash_x, last = state
     final_row = final_gain[None, :]
-    mine = embed(last, final_row, positive)[:4]
     count = lax.axis_size(DP)
-    copies = jnp.broadcast_to(mine, (count, *mine.shape))
+    copies = embed(count, last, final_row, positive)
     everyone = lax.all_to_all(copies, DP, split_axis=0, concat_axis=0, tiled=True)
-    everyone = everyone.reshape(count * 4, D + 128)
+    everyone = everyone.reshape(count * 8, WIDE)
     seed = loss_seed(replica.reshape(1), last, final_row, everyone)
     grads = jnp.zeros((rows, D), BF16)
     for tick in range(ticks):
         out, grads = backward_layer(
-            tick, stages - 1, micro, meta, inbox, seed, gain, table, packed, full_out,
+            tick, stages - 1, micro, meta, inbox, seed, gain, table, wq, wo,
             (stash_h, stash_x), grads,
         )
         if tick < ticks - 1:

time: 545 us -> 528 us (0.969)
  the two profiles are of different devices: /device:TPU:2 before, /device:TPU:1 now
where the time goes in v2:
time: 528 us; the launch traced here: 522 us
  waiting for transfers between devices  365 us (69%)
  Pallas kernels  91.9 us (17%)
  starting transfers between devices  31.4 us (6%)
  local copies, waits for them, and re-layouts  19.3 us (4%)
  between operations  14.4 us (3%)
    ppermute x20, waiting for transfers between devices, per_device(): inbox = lax.ppermute(out, 'section', pairs)  272 us
    all_gather x1, waiting for transfers between devices, per_device(): lax.all_gather(pack(w_qkv[0], w_out[0]), DP, axis=0, tiled=True)  76.5 us
    pallas_call x11, Pallas kernels, forward_layer(): pl.pallas_call(functools.partial(forward_kernel, tick, last_stage, micro)...  42.5 us
    pallas_call x11, Pallas kernels, backward_layer(): pl.pallas_call(functools.partial(backward_kernel, tick, last_stage, micro...  42.4 us
    ppermute x20, starting transfers between devices, per_device(): inbox = lax.ppermute(out, 'section', pairs)  26.2 us
    unnamed x36, local copies, waits for them, and re-layouts  17.2 us
    all_to_all x1, waiting for transfers between devices, per_device(): lax.all_to_all(copies, DP, split_axis=0, concat_axis=0, tiled=True)  16.2 us
  transfers between devices with their start and end apart: 22, of which 10 were waited for; matrix products, arithmetic and copies ran while one was open for 0% of the time, Pallas kernels for 0%

profile of v2, /device:TPU:1, one launch (start us, length us, event | category | flops | bytes accessed | tf_op | source)
XLA Modules:
  0.0 521.9 jit_solution(16420973415531065752)
XLA Ops:
  10.4 76.5 %all-gather.2.cloned.1.call-done.packed = bf16[3584,2048]{1,0:T(8,128)(2,1)} async-done(((bf16[112,2048]{1,0:T(8,128)(2,1)}), bf16[3584,2048]{1,0:T(8,128)(2,1)}) %all-gather.2.cloned.1.call-update) | async-done | bytes 14680080 | tf_op jit(solution)/shard_map/all_gather | solution.py:534
  86.9 5.2 copy-done.7
  96.4 10.2 %forward_layer.11 = (bf16[48,3584]{1,0:T(8,128)(2,1)S(1)}, bf16[192,3584]{1,0:T(8,128)(2,1)S(1)}, bf16[192,1152]{1,0:T(8,128)(2,1)S(1)}, f32[4,8,3584]{2,1,0:T(8,128)S(1)}) custom-call(s32[6]{0:T(128)S(1)} %pad_add_fusion.meta, bf16[48,3584]{1,0:T(8,128)(2,1)S(1)} %copy-done.10, ...), custom_call_target="tpu_custom_call", output_to_operand_aliasing={{1}: (7, {}), {2}: (8, {}), {3}: (9, {})} | custom-call | flops 704643072 | bytes 14680064 | tf_op jit(solution)/shard_map/forward_layer/pallas_call | solution.py:319
  107.9 4.2 collective-permute-done.inbox
  112.1 6.0 %forward_layer.12 = (bf16[48,3584]{1,0:T(8,128)(2,1)S(1)}, bf16[192,3584]{1,0:T(8,128)(2,1)S(1)}, bf16[192,1152]{1,0:T(8,128)(2,1)S(1)}, f32[4,8,3584]{2,1,0:T(8,128)S(1)}) custom-call(s32[6]{0:T(128)S(1)} %pad_add_fusion.meta, bf16[48,3584]{1,0:T(8,128)(2,1)S(1)} %collective-permute-done.inbox, ...), custom_call_target="tpu_custom_call", output_to_operand_aliasing={{1}: (7, {}), {2}: (8, {}), {3}: (9, {})} | custom-call | flops 704643072 | bytes 14680064 | tf_op jit(solution)/shard_map/forward_layer/pallas_call | solution.py:319
  118.1 3.8 collective-permute-start.1
  121.9 5.2 %collective-permute-done.1.inbox = bf16[48,3584]{1,0:T(8,128)(2,1)S(1)} collective-permute-done((bf16[48,3584]{1,0:T(8,128)(2,1)S(1)}, bf16[48,3584]{1,0:T(8,128)(2,1)S(1)}, u32[]{:S(2)}, u32[]{:S(2)}) %collective-permute-start.1) | collective-permute-done | bytes 344096 | tf_op jit(solution)/shard_map/ppermute | solution.py:552
  127.2 6.0 %forward_layer.13 = (bf16[48,3584]{1,0:T(8,128)(2,1)S(1)}, bf16[192,3584]{1,0:T(8,128)(2,1)S(1)}, bf16[192,1152]{1,0:T(8,128)(2,1)S(1)}, f32[4,8,3584]{2,1,0:T(8,128)S(1)}) custom-call(s32[6]{0:T(128)S(1)} %pad_add_fusion.meta, bf16[48,3584]{1,0:T(8,128)(2,1)S(1)} %collective-permute-done.1.inbox, ...), custom_call_target="tpu_custom_call", output_to_operand_aliasing={{1}: (7, {}), {2}: (8, {}), {3}: (9, {})} | custom-call | flops 704643072 | bytes 14680064 | tf_op jit(solution)/shard_map/forward_layer/pallas_call | solution.py:319
  133.2 3.8 collective-permute-start.2
  137.0 6.4 %collective-permute-done.2.inbox = bf16[48,3584]{1,0:T(8,128)(2,1)S(1)} collective-permute-done((bf16[48,3584]{1,0:T(8,128)(2,1)S(1)}, bf16[48,3584]{1,0:T(8,128)(2,1)S(1)}, u32[]{:S(2)}, u32[]{:S(2)}) %collective-permute-start.2) | collective-permute-done | bytes 344096 | tf_op jit(solution)/shard_map/ppermute | solution.py:552
  143.4 6.0 %forward_layer.14 = (bf16[48,3584]{1,0:T(8,128)(2,1)S(1)}, bf16[192,3584]{1,0:T(8,128)(2,1)S(1)}, bf16[192,1152]{1,0:T(8,128)(2,1)S(1)}, f32[4,8,3584]{2,1,0:T(8,128)S(1)}) custom-call(s32[6]{0:T(128)S(1)} %pad_add_fusion.meta, bf16[48,3584]{1,0:T(8,128)(2,1)S(1)} %collective-permute-done.2.inbox, ...), custom_call_target="tpu_custom_call", output_to_operand_aliasing={{1}: (7, {}), {2}: (8, {}), {3}: (9, {})} | custom-call | flops 704643072 | bytes 14680064 | tf_op jit(solution)/shard_map/forward_layer/pallas_call | solution.py:319
  149.4 3.8 collective-permute-start.3
  153.3 7.5 %collective-permute-done.3.inbox = bf16[48,3584]{1,0:T(8,128)(2,1)S(1)} collective-permute-done((bf16[48,3584]{1,0:T(8,128)(2,1)S(1)}, bf16[48,3584]{1,0:T(8,128)(2,1)S(1)}, u32[]{:S(2)}, u32[]{:S(2)}) %collective-permute-start.3) | collective-permute-done | bytes 344096 | tf_op jit(solution)/shard_map/ppermute | solution.py:552
  166.0 10.0 %forward_layer.19 = (bf16[48,3584]{1,0:T(8,128)(2,1)S(1)}, bf16[192,3584]{1,0:T(8,128)(2,1)S(1)}, bf16[192,1152]{1,0:T(8,128)(2,1)S(1)}, f32[4,8,3584]{2,1,0:T(8,128)S(1)}) custom-call(s32[6]{0:T(128)S(1)} %pad_add_fusion.meta, bf16[48,3584]{1,0:T(8,128)(2,1)S(1)} %collective-permute-done.7.inbox, ...), custom_call_target="tpu_custom_call", output_to_operand_aliasing={{1}: (7, {}), {2}: (8, {}), {3}: (9, {})} | custom-call | flops 704643072 | bytes 14680064 | tf_op jit(solution)/shard_map/forward_layer/pallas_call | solution.py:319
  182.0 5.3 %all-to-all-start = ((bf16[32,8,1920]{2,1,0:T(8,128)(2,1)}), bf16[32,8,1920]{2,1,0:T(8,128)(2,1)S(1)}, u32[]{:S(2)}, u32[]{:S(2)}) async-start(bf16[32,8,1920]{2,1,0:T(8,128)(2,1)} %copy-done.9), calls=%async_computation | async-start | bytes 1966080 | tf_op jit(solution)/shard_map/all_to_all | solution.py:557
  187.3 16.2 %all-to-all-done = bf16[32,8,1920]{2,1,0:T(8,128)(2,1)S(1)} async-done(((bf16[32,8,1920]{2,1,0:T(8,128)(2,1)}), bf16[32,8,1920]{2,1,0:T(8,128)(2,1)S(1)}, u32[]{:S(2)}, u32[]{:S(2)}) %all-to-all-start) | async-done | bytes 983072 | tf_op jit(solution)/shard_map/all_to_all | solution.py:557
  224.0 222.7 %collective-permute-done.16.inbox = bf16[48,3584]{1,0:T(8,128)(2,1)S(1)} collective-permute-done((bf16[48,3584]{1,0:T(8,128)(2,1)S(1)}, bf16[48,3584]{1,0:T(8,128)(2,1)S(1)}, u32[]{:S(2)}, u32[]{:S(2)}) %collective-permute-start.16) | collective-permute-done | bytes 344096 | tf_op jit(solution)/shard_map/ppermute | solution.py:572
  446.7 9.4 %backward_layer.18 = (bf16[48,3584]{1,0:T(8,128)(2,1)S(1)}, bf16[192,3584]{1,0:T(8,128)(2,1)}) custom-call(s32[6]{0:T(128)S(1)} %pad_add_fusion.meta, bf16[48,3584]{1,0:T(8,128)(2,1)S(1)} %collective-permute-done.16.inbox, f32[8,3584]{1,0:T(8,128)S(1)} %loss_seed.1.seed, f32[1,3584]{1,0:T(1,128)S(1)} %copy-done.8, ...), custom_call_target="tpu_custom_call", output_to_operand_aliasing={{1}: (9, {})} | custom-call | flops 704643072 | bytes 14680064 | tf_op jit(solution)/shard_map/backward_layer/pallas_call | solution.py:346
  457.4 10.1 %collective-permute-done.17.inbox = bf16[48,3584]{1,0:T(8,128)(2,1)S(1)} collective-permute-done((bf16[48,3584]{1,0:T(8,128)(2,1)S(1)}, bf16[48,3584]{1,0:T(8,128)(2,1)S(1)}, u32[]{:S(2)}, u32[]{:S(2)}) %collective-permute-start.17) | collective-permute-done | bytes 344096 | tf_op jit(solution)/shard_map/ppermute | solution.py:572
  467.5 9.3 %backward_layer.19 = (bf16[48,3584]{1,0:T(8,128)(2,1)S(1)}, bf16[192,3584]{1,0:T(8,128)(2,1)}) custom-call(s32[6]{0:T(128)S(1)} %pad_add_fusion.meta, bf16[48,3584]{1,0:T(8,128)(2,1)S(1)} %collective-permute-done.17.inbox, f32[8,3584]{1,0:T(8,128)S(1)} %loss_seed.1.seed, f32[1,3584]{1,0:T(1,128)S(1)} %copy-done.8, ...), custom_call_target="tpu_custom_call", output_to_operand_aliasing={{1}: (9, {})} | custom-call | flops 704643072 | bytes 14680064 | tf_op jit(solution)/shard_map/backward_layer/pallas_call | solution.py:346
  478.2 8.5 %collective-permute-done.18.inbox = bf16[48,3584]{1,0:T(8,128)(2,1)S(1)} collective-permute-done((bf16[48,3584]{1,0:T(8,128)(2,1)S(1)}, bf16[48,3584]{1,0:T(8,128)(2,1)S(1)}, u32[]{:S(2)}, u32[]{:S(2)}) %collective-permute-start.18) | collective-permute-done | bytes 344096 | tf_op jit(solution)/shard_map/ppermute | solution.py:572
  486.7 9.3 %backward_layer.20 = (bf16[48,3584]{1,0:T(8,128)(2,1)S(1)}, bf16[192,3584]{1,0:T(8,128)(2,1)}) custom-call(s32[6]{0:T(128)S(1)} %pad_add_fusion.meta, bf16[48,3584]{1,0:T(8,128)(2,1)S(1)} %collective-permute-done.18.inbox, f32[8,3584]{1,0:T(8,128)S(1)} %loss_seed.1.seed, f32[1,3584]{1,0:T(1,128)S(1)} %copy-done.8, ...), custom_call_target="tpu_custom_call", output_to_operand_aliasing={{1}: (9, {})} | custom-call | flops 704643072 | bytes 14680064 | tf_op jit(solution)/shard_map/backward_layer/pallas_call | solution.py:346
  497.3 7.2 %collective-permute-done.19.inbox = bf16[48,3584]{1,0:T(8,128)(2,1)S(1)} collective-permute-done((bf16[48,3584]{1,0:T(8,128)(2,1)S(1)}, bf16[48,3584]{1,0:T(8,128)(2,1)S(1)}, u32[]{:S(2)}, u32[]{:S(2)}) %collective-permute-start.19) | collective-permute-done | bytes 344096 | tf_op jit(solution)/shard_map/ppermute | solution.py:572
  504.5 10.1 %backward_layer.21 = (bf16[48,3584]{1,0:T(8,128)(2,1)}, bf16[192,3584]{1,0:T(8,128)(2,1)}) custom-call(s32[6]{0:T(128)S(1)} %pad_add_fusion.meta, bf16[48,3584]{1,0:T(8,128)(2,1)S(1)} %collective-permute-done.19.inbox, f32[8,3584]{1,0:T(8,128)S(1)} %loss_seed.1.seed, f32[1,3584]{1,0:T(1,128)S(1)} %copy-done.8, ...), custom_call_target="tpu_custom_call", output_to_operand_aliasing={{1}: (9, {})} | custom-call | flops 704643072 | bytes 14680064 | tf_op jit(solution)/shard_map/backward_layer/pallas_call | solution.py:346
  (93 shorter events, 44.6 us)
Async XLA Ops:
  6.5 80.3 %all-gather.2.cloned.1.call-start = ((), (), s32[]{:S(2)}) async-start(), calls=%async_computation.1 | async-start | bytes 15138816 | tf_op jit(solution)/shard_map/all_gather | solution.py:534
  95.1 83.0 %copy-start = (bf16[3584,1152]{1,0:T(8,128)(2,1)}, bf16[3584,1152]{1,0:T(8,128)(2,1)S(1)}, u32[]{:S(2)}) copy-start(bf16[3584,1152]{1,0:T(8,128)(2,1)S(1)} %get-tuple-element.71.wq) | copy-start | bytes 24772612
  95.1 83.0 %copy-start.2 = (bf16[896,3584]{1,0:T(8,128)(2,1)}, bf16[896,3584]{1,0:T(8,128)(2,1)S(1)}, u32[]{:S(2)}) copy-start(bf16[896,3584]{1,0:T(8,128)(2,1)S(1)} %get-tuple-element.72.wo) | copy-start | bytes 19267588
  106.6 5.5 %collective-permute-start = (bf16[48,3584]{1,0:T(8,128)(2,1)S(1)}, bf16[48,3584]{1,0:T(8,128)(2,1)S(1)}, u32[]{:S(2)}, u32[]{:S(2)}) collective-permute-start(bf16[48,3584]{1,0:T(8,128)(2,1)S(1)} %get-tuple-element.73), channel_id=1, source_target_pairs={{0,32},{1,33},{2,34},{3,35},{4,36},{5,37},{6,38},{7,39},{8,40},{9,... | collective-permute-start | bytes 1032200 | tf_op jit(solution)/shard_map/ppermute | solution.py:552
  118.1 9.1 %collective-permute-start.1 = (bf16[48,3584]{1,0:T(8,128)(2,1)S(1)}, bf16[48,3584]{1,0:T(8,128)(2,1)S(1)}, u32[]{:S(2)}, u32[]{:S(2)}) collective-permute-start(bf16[48,3584]{1,0:T(8,128)(2,1)S(1)} %get-tuple-element.77), channel_id=1, source_target_pairs={{0,32},{32,64},{1,33},{33,65},{2,34},{34,66},{3,35},{35,67},{4,36}... | collective-permute-start | bytes 1032200 | tf_op jit(solution)/shard_map/ppermute | solution.py:552
  133.2 10.2 %collective-permute-start.2 = (bf16[48,3584]{1,0:T(8,128)(2,1)S(1)}, bf16[48,3584]{1,0:T(8,128)(2,1)S(1)}, u32[]{:S(2)}, u32[]{:S(2)}) collective-permute-start(bf16[48,3584]{1,0:T(8,128)(2,1)S(1)} %get-tuple-element.81), channel_id=1, source_target_pairs={{0,32},{32,64},{64,96},{1,33},{33,65},{65,97},{2,34},{34,66},{66,9... | collective-permute-start | bytes 1032200 | tf_op jit(solution)/shard_map/ppermute | solution.py:552
  149.4 11.4 %collective-permute-start.3 = (bf16[48,3584]{1,0:T(8,128)(2,1)S(1)}, bf16[48,3584]{1,0:T(8,128)(2,1)S(1)}, u32[]{:S(2)}, u32[]{:S(2)}) collective-permute-start(bf16[48,3584]{1,0:T(8,128)(2,1)S(1)} %get-tuple-element.85), channel_id=1, source_target_pairs={{0,32},{32,64},{64,96},{96,128},{1,33},{33,65},{65,97},{97,129},{2... | collective-permute-start | bytes 1032200 | tf_op jit(solution)/shard_map/ppermute | solution.py:552
  161.4 0.7 collective-permute-start.4
  162.7 0.7 collective-permute-start.5
  164.0 0.7 collective-permute-start.6
  165.3 0.7 collective-permute-start.7
  176.0 0.7 collective-permute-start.8
  177.3 0.7 collective-permute-start.9
  182.0 21.5 %all-to-all-start = ((bf16[32,8,1920]{2,1,0:T(8,128)(2,1)}), bf16[32,8,1920]{2,1,0:T(8,128)(2,1)S(1)}, u32[]{:S(2)}, u32[]{:S(2)}) async-start(bf16[32,8,1920]{2,1,0:T(8,128)(2,1)} %copy-done.9), calls=%async_computation | async-start | bytes 1966080 | tf_op jit(solution)/shard_map/all_to_all | solution.py:557
  214.8 0.7 collective-permute-start.10
  216.1 0.7 collective-permute-start.11
  217.4 0.7 collective-permute-start.12
  218.7 0.7 collective-permute-start.13
  220.2 0.7 collective-permute-start.14
  221.4 0.7 collective-permute-start.15
  222.7 224.0 %collective-permute-start.16 = (bf16[48,3584]{1,0:T(8,128)(2,1)S(1)}, bf16[48,3584]{1,0:T(8,128)(2,1)S(1)}, u32[]{:S(2)}, u32[]{:S(2)}) collective-permute-start(bf16[48,3584]{1,0:T(8,128)(2,1)S(1)} %get-tuple-element.128), channel_id=1, source_target_pairs={{128,96},{96,64},{64,32},{32,0},{129,97},{97,65},{65,33},{33,1},{1... | collective-permute-start | bytes 1032200 | tf_op jit(solution)/shard_map/ppermute | solution.py:572
  456.1 11.4 %collective-permute-start.17 = (bf16[48,3584]{1,0:T(8,128)(2,1)S(1)}, bf16[48,3584]{1,0:T(8,128)(2,1)S(1)}, u32[]{:S(2)}, u32[]{:S(2)}) collective-permute-start(bf16[48,3584]{1,0:T(8,128)(2,1)S(1)} %get-tuple-element.130), channel_id=1, source_target_pairs={{96,64},{64,32},{32,0},{97,65},{65,33},{33,1},{98,66},{66,34},{34,... | collective-permute-start | bytes 1032200 | tf_op jit(solution)/shard_map/ppermute | solution.py:572
  476.9 9.8 %collective-permute-start.18 = (bf16[48,3584]{1,0:T(8,128)(2,1)S(1)}, bf16[48,3584]{1,0:T(8,128)(2,1)S(1)}, u32[]{:S(2)}, u32[]{:S(2)}) collective-permute-start(bf16[48,3584]{1,0:T(8,128)(2,1)S(1)} %get-tuple-element.132), channel_id=1, source_target_pairs={{64,32},{32,0},{65,33},{33,1},{66,34},{34,2},{67,35},{35,3},{68,36... | collective-permute-start | bytes 1032200 | tf_op jit(solution)/shard_map/ppermute | solution.py:572
  496.0 8.5 %collective-permute-start.19 = (bf16[48,3584]{1,0:T(8,128)(2,1)S(1)}, bf16[48,3584]{1,0:T(8,128)(2,1)S(1)}, u32[]{:S(2)}, u32[]{:S(2)}) collective-permute-start(bf16[48,3584]{1,0:T(8,128)(2,1)S(1)} %get-tuple-element.134), channel_id=1, source_target_pairs={{32,0},{33,1},{34,2},{35,3},{36,4},{37,5},{38,6},{39,7},{40,8},{41... | collective-permute-start | bytes 1032200 | tf_op jit(solution)/shard_map/ppermute | solution.py:572
  (16 other events, 30.1 us)
Sparse Core Ops, SparseCore 0:
  9.9 76.9 all-gather.1

commit v3 on v2

--- a/solution.py
+++ b/solution.py
@@ -21,9 +21,9 @@
 EPS = 1e-06
 SHARP = 20.0
 COEF = 256.0
-CHUNK = 512
-CHUNKS = D // CHUNK
-STAGGER = 4200
+HALVES = 2
+HALF = D // HALVES
+STAGGER = 6500
 F32 = jnp.float32
 BF16 = jnp.bfloat16
 
@@ -154,7 +154,7 @@
 
         if tick == 0:
 
-            @pl.when(meta[1 + micro] == 1)
+            @pl.when(meta[5] == 1)
             def _():
                 pl.delay(STAGGER)
 
@@ -163,13 +163,7 @@
         keep_h.start()
         wide = h_v[...].astype(F32)
         n_v[...] = (wide * inv_rms(wide) * gain[...]).astype(BF16)
-        acc_v[...] = jnp.zeros_like(acc_v)
-
-        @pl.loop(0, CHUNKS)
-        def _(i):
-            cols = pl.ds(pl.multiple_of(i * CHUNK, CHUNK), CHUNK)
-            acc_v[...] += dot_nn(n_v[:, cols], wq[cols, :])
-
+        acc_v[...] = dot_nn(n_v[...], wq[...])
         cosine, sine = table[0], table[1]
         for i in range(PAIRS + 1):
             part = acc_v[:, 128 * i : 128 * i + 128]
@@ -184,9 +178,9 @@
         for i in range(PAIRS):
             ctx_v[:, 128 * i : 128 * i + 128] = context[LEN * i : LEN * i + LEN]
 
-        @pl.loop(0, CHUNKS)
+        @pl.loop(0, HALVES)
         def _(i):
-            cols = pl.ds(pl.multiple_of(i * CHUNK, CHUNK), CHUNK)
+            cols = pl.ds(pl.multiple_of(i * HALF, HALF), HALF)
             branch = dot_nn(ctx_v[...], wo[:, cols])
             out[:, cols] = (h_v[:, cols].astype(F32) + branch).astype(BF16)
 
@@ -242,7 +236,7 @@
         get_h.start()
         if tick == 0:
 
-            @pl.when(meta[1 + micro] == 1)
+            @pl.when(meta[5] == 1)
             def _():
                 pl.delay(STAGGER)
 
@@ -258,13 +252,7 @@
         def _():
             g_v[...] = inbox[...]
 
-        dctx_v[...] = jnp.zeros_like(dctx_v)
-
-        @pl.loop(0, CHUNKS)
-        def _(i):
-            cols = pl.ds(pl.multiple_of(i * CHUNK, CHUNK), CHUNK)
-            dctx_v[...] += dot_nt(g_v[:, cols], wo[:, cols])
-
+        dctx_v[...] = dot_nt(g_v[...], wo[...])
         get_x.wait()
         q_rows = rows_of(x_v)
         k_blocks = paired(x_v[:, QW : QW + KV].astype(F32))
@@ -285,9 +273,9 @@
         dx_v[:, QW : QW + KV] = (dkey * cosine - partner(dkey) * sine).astype(BF16)
         dx_v[:, QW + KV :] = dvalue.astype(BF16)
 
-        @pl.loop(0, CHUNKS)
+        @pl.loop(0, HALVES)
         def _(i):
-            rows = pl.ds(pl.multiple_of(i * CHUNK, CHUNK), CHUNK)
+            rows = pl.ds(pl.multiple_of(i * HALF, HALF), HALF)
             dn_v[:, rows] = dot_nt(dx_v[...], wq[rows, :]).astype(BF16)
 
         get_h.wait()
@@ -426,7 +414,6 @@
     )(packed)
 
 
-HALF = D // 2
 WIDE = HALF + 128
 
 
@@ -434,7 +421,8 @@
     return jnp.concatenate([last[j, 0:1, :] for j in (0, 2, 1, 3)], axis=0)
 
 
-def embed_kernel(last, final_gain, labels, out):
+def embed_kernel(last, final_gain, labels, wq, wo, out):
+    del wq, wo
     rows = pooled_rows(last)
     pooled = rows * inv_rms(rows) * final_gain[...]
     unit = pooled * lax.rsqrt(jnp.sum(pooled * pooled, axis=1, keepdims=True))
@@ -447,18 +435,19 @@
         out[i, :, HALF:] = label
 
 
-def embed(count, last, final_gain, labels):
+def embed(count, last, final_gain, labels, wq, wo):
     return pl.pallas_call(
         functools.partial(embed_kernel),
         out_shape=jax.ShapeDtypeStruct((count, 8, WIDE), BF16),
-        in_specs=[VMEM, VMEM, SMEM],
+        in_specs=[VMEM, VMEM, SMEM, VMEM, VMEM],
         out_specs=VMEM,
-        compiler_params=pltpu.CompilerParams(vmem_limit_bytes=SMALL),
+        compiler_params=pltpu.CompilerParams(vmem_limit_bytes=LIMIT),
         name="embed",
-    )(last, final_gain, labels)
-
-
-def loss_kernel(me, last, final_gain, everyone, seed):
+    )(last, final_gain, labels, wq, wo)
+
+
+def loss_kernel(me, last, final_gain, everyone, wq, wo, seed):
+    del wq, wo
     count = everyone.shape[0]
     emb = everyone[:, :HALF]
     label = everyone[:, HALF:].astype(F32)[:, 0:1].astype(jnp.int32)
@@ -475,7 +464,7 @@
     coef = jnp.where(valid, (prob - (col == target).astype(F32)) * (COEF * SHARP), 0.0)
     both = coef + coef.T
     mine = lax.broadcasted_iota(jnp.int32, (8, count), 0)
-    pick = lax.broadcasted_iota(jnp.int32, (8, count), 1) == me[0] * 8 + mine
+    pick = lax.broadcasted_iota(jnp.int32, (8, count), 1) == me[6] * 8 + mine
     own = lax.dot_general(
         pick.astype(F32),
         both,
@@ -506,15 +495,15 @@
     )
 
 
-def loss_seed(me, last, final_gain, everyone):
+def loss_seed(me, last, final_gain, everyone, wq, wo):
     return pl.pallas_call(
         loss_kernel,
         out_shape=jax.ShapeDtypeStruct((8, D), F32),
-        in_specs=[SMEM, VMEM, VMEM, VMEM],
+        in_specs=[SMEM, VMEM, VMEM, VMEM, VMEM, VMEM],
         out_specs=VMEM,
-        compiler_params=pltpu.CompilerParams(vmem_limit_bytes=SMALL),
+        compiler_params=pltpu.CompilerParams(vmem_limit_bytes=LIMIT),
         name="loss_seed",
-    )(me, last, final_gain, everyone)
+    )(me, last, final_gain, everyone, wq, wo)
 
 
 def rotary_table():
@@ -531,8 +520,11 @@
     replica = lax.axis_index(DP)
     micro = lengths.shape[0]
     core = lax.axis_index("dp_2")
-    wq, wo = unpack(lax.all_gather(pack(w_qkv[0], w_out[0]), DP, axis=0, tiled=True))
-    meta = jnp.concatenate([stage.reshape(1), lengths, core.reshape(1)]).astype(jnp.int32)
+    meta = jnp.concatenate([stage[None], lengths, core[None], replica[None]])
+    shard, final_row, meta = lax.optimization_barrier(
+        (pack(w_qkv[0], w_out[0]), final_gain[None, :], meta)
+    )
+    wq, wo = unpack(lax.all_gather(shard, DP, axis=0, tiled=True))
     table = rotary_table()
     gain = norm_gain
     ticks = micro + stages - 1
@@ -551,12 +543,11 @@
             pairs = [(s, s + 1) for s in range(stages - 1) if 0 <= tick - s < micro]
             inbox = lax.ppermute(out, "section", pairs)
     stash_h, stash_x, last = state
-    final_row = final_gain[None, :]
     count = lax.axis_size(DP)
-    copies = embed(count, last, final_row, positive)
+    copies = embed(count, last, final_row, positive, wq, wo)
     everyone = lax.all_to_all(copies, DP, split_axis=0, concat_axis=0, tiled=True)
     everyone = everyone.reshape(count * 8, WIDE)
-    seed = loss_seed(replica.reshape(1), last, final_row, everyone)
+    seed = loss_seed(meta, last, final_row, everyone, wq, wo)
     grads = jnp.zeros((rows, D), BF16)
     for tick in range(ticks):
         out, grads = backward_layer(

time: 528 us -> 481 us (0.911)
  the two profiles are of different devices: /device:TPU:1 before, /device:TPU:8 now
where the time goes in v3:
time: 481 us; the launch traced here: 471 us
  waiting for transfers between devices  320 us (67%)
  Pallas kernels  75.3 us (16%)
  starting transfers between devices  27.9 us (6%)
  blocking collectives  23 us (5%)
  between operations  14.5 us (3%)
  local copies, waits for them, and re-layouts  9.78 us (2%)
    ppermute x20, waiting for transfers between devices, per_device(): inbox = lax.ppermute(out, 'section', pairs)  244 us
    all_gather x1, waiting for transfers between devices, per_device(): wq, wo = unpack(lax.all_gather(shard, DP, axis=0, tiled=True))  75.2 us
    pallas_call x11, Pallas kernels, backward_layer(): pl.pallas_call(functools.partial(backward_kernel, tick, last_stage, micro...  45.2 us
    ppermute x20, starting transfers between devices, per_device(): inbox = lax.ppermute(out, 'section', pairs)  27.9 us
    all_to_all x1, blocking collectives, per_device(): lax.all_to_all(copies, DP, split_axis=0, concat_axis=0, tiled=True)  23 us
    pallas_call x11, Pallas kernels, forward_layer(): pl.pallas_call(functools.partial(forward_kernel, tick, last_stage, micro)...  22.6 us
  transfers between devices with their start and end apart: 21, of which 9 were waited for; matrix products, arithmetic and copies ran while one was open for 0% of the time, Pallas kernels for 0%

profile of v3, /device:TPU:8, one launch (start us, length us, event | category | flops | bytes accessed | tf_op | source)
XLA Modules:
  0.0 471.0 jit_solution(17705279668709790286)
XLA Ops:
  11.0 75.2 %all-gather.2.cloned.1.call-done.packed = bf16[3584,2048]{1,0:T(8,128)(2,1)} async-done(((bf16[112,2048]{1,0:T(8,128)(2,1)}), bf16[3584,2048]{1,0:T(8,128)(2,1)}) %all-gather.2.cloned.1.call-update) | async-done | bytes 14680080 | tf_op jit(solution)/shard_map/all_gather | solution.py:527
  86.3 5.2 %copy-done.1 = bf16[3584,2048]{1,0:T(8,128)(2,1)S(1)} copy-done((bf16[3584,2048]{1,0:T(8,128)(2,1)S(1)}, bf16[3584,2048]{1,0:T(8,128)(2,1)}, u32[]{:S(2)}) %copy-start.1) | copy-done | bytes 14680088
  91.5 3.0 unpack.1
  95.2 4.3 forward_layer.11
  100.8 4.7 %collective-permute-done.inbox = bf16[48,3584]{1,0:T(8,128)(2,1)S(1)} collective-permute-done((bf16[48,3584]{1,0:T(8,128)(2,1)S(1)}, bf16[48,3584]{1,0:T(8,128)(2,1)S(1)}, u32[]{:S(2)}, u32[]{:S(2)}) %collective-permute-start) | collective-permute-done | bytes 344096 | tf_op jit(solution)/shard_map/ppermute | solution.py:544
  105.5 4.3 forward_layer.12
  109.9 4.4 collective-permute-start.1
  114.3 4.7 %collective-permute-done.1.inbox = bf16[48,3584]{1,0:T(8,128)(2,1)S(1)} collective-permute-done((bf16[48,3584]{1,0:T(8,128)(2,1)S(1)}, bf16[48,3584]{1,0:T(8,128)(2,1)S(1)}, u32[]{:S(2)}, u32[]{:S(2)}) %collective-permute-start.1) | collective-permute-done | bytes 344096 | tf_op jit(solution)/shard_map/ppermute | solution.py:544
  119.0 4.3 forward_layer.13
  123.3 4.4 collective-permute-start.2
  127.7 4.7 %collective-permute-done.2.inbox = bf16[48,3584]{1,0:T(8,128)(2,1)S(1)} collective-permute-done((bf16[48,3584]{1,0:T(8,128)(2,1)S(1)}, bf16[48,3584]{1,0:T(8,128)(2,1)S(1)}, u32[]{:S(2)}, u32[]{:S(2)}) %collective-permute-start.2) | collective-permute-done | bytes 344096 | tf_op jit(solution)/shard_map/ppermute | solution.py:544
  132.4 4.3 forward_layer.14
  136.8 4.4 collective-permute-start.3
  141.2 5.8 %collective-permute-done.3.inbox = bf16[48,3584]{1,0:T(8,128)(2,1)S(1)} collective-permute-done((bf16[48,3584]{1,0:T(8,128)(2,1)S(1)}, bf16[48,3584]{1,0:T(8,128)(2,1)S(1)}, u32[]{:S(2)}, u32[]{:S(2)}) %collective-permute-start.3) | collective-permute-done | bytes 344096 | tf_op jit(solution)/shard_map/ppermute | solution.py:544
  157.5 23.0 %all_to_all.5 = bf16[32,8,1920]{2,1,0:T(8,128)(2,1)S(1)} all-to-all(bf16[32,8,1920]{2,1,0:T(8,128)(2,1)S(1)} %embed.1), channel_id=1, replica_groups=mesh['section'=8,'dp_0'=4,'dp_1'=4,'dp_2'=2] {'dp_0','dp_1','dp_2'}, dimensions={0} | all-to-all | bytes 1966080 | tf_op jit(solution)/shard_map/all_to_all | solution.py:548
  188.5 9.0 %backward_layer.14 = (bf16[48,3584]{1,0:T(8,128)(2,1)S(1)}, bf16[192,3584]{1,0:T(8,128)(2,1)}) custom-call(s32[7]{0:T(128)S(1)} %pad_add_fusion.meta.me, bf16[48,3584]{1,0:T(8,128)(2,1)S(1)} %collective-permute-done.12.inbox, f32[8,3584]{1,0:T(8,128)S(1)} %loss_seed.1.seed, f32[1,3584]{1,0:T(1,128)S(1)} %copy-done.2, ...), custom_call_target="tpu_custom_call", output_to_operand_aliasing={{1}: (9, {})} | custom-call | flops 704643072 | bytes 14680064 | tf_op jit(solution)/shard_map/backward_layer/pallas_call | solution.py:334
  202.6 190.9 %collective-permute-done.16.inbox = bf16[48,3584]{1,0:T(8,128)(2,1)S(1)} collective-permute-done((bf16[48,3584]{1,0:T(8,128)(2,1)S(1)}, bf16[48,3584]{1,0:T(8,128)(2,1)S(1)}, u32[]{:S(2)}, u32[]{:S(2)}) %collective-permute-start.16) | collective-permute-done | bytes 344096 | tf_op jit(solution)/shard_map/ppermute | solution.py:563
  393.5 7.9 %backward_layer.18 = (bf16[48,3584]{1,0:T(8,128)(2,1)S(1)}, bf16[192,3584]{1,0:T(8,128)(2,1)}) custom-call(s32[7]{0:T(128)S(1)} %pad_add_fusion.meta.me, bf16[48,3584]{1,0:T(8,128)(2,1)S(1)} %collective-permute-done.16.inbox, f32[8,3584]{1,0:T(8,128)S(1)} %loss_seed.1.seed, f32[1,3584]{1,0:T(1,128)S(1)} %copy-done.2, ...), custom_call_target="tpu_custom_call", output_to_operand_aliasing={{1}: (9, {})} | custom-call | flops 704643072 | bytes 14680064 | tf_op jit(solution)/shard_map/backward_layer/pallas_call | solution.py:334
  402.6 13.0 %collective-permute-done.17.inbox = bf16[48,3584]{1,0:T(8,128)(2,1)S(1)} collective-permute-done((bf16[48,3584]{1,0:T(8,128)(2,1)S(1)}, bf16[48,3584]{1,0:T(8,128)(2,1)S(1)}, u32[]{:S(2)}, u32[]{:S(2)}) %collective-permute-start.17) | collective-permute-done | bytes 344096 | tf_op jit(solution)/shard_map/ppermute | solution.py:563
  415.6 8.4 %backward_layer.19 = (bf16[48,3584]{1,0:T(8,128)(2,1)S(1)}, bf16[192,3584]{1,0:T(8,128)(2,1)}) custom-call(s32[7]{0:T(128)S(1)} %pad_add_fusion.meta.me, bf16[48,3584]{1,0:T(8,128)(2,1)S(1)} %collective-permute-done.17.inbox, f32[8,3584]{1,0:T(8,128)S(1)} %loss_seed.1.seed, f32[1,3584]{1,0:T(1,128)S(1)} %copy-done.2, ...), custom_call_target="tpu_custom_call", output_to_operand_aliasing={{1}: (9, {})} | custom-call | flops 704643072 | bytes 14680064 | tf_op jit(solution)/shard_map/backward_layer/pallas_call | solution.py:334
  425.4 11.2 %collective-permute-done.18.inbox = bf16[48,3584]{1,0:T(8,128)(2,1)S(1)} collective-permute-done((bf16[48,3584]{1,0:T(8,128)(2,1)S(1)}, bf16[48,3584]{1,0:T(8,128)(2,1)S(1)}, u32[]{:S(2)}, u32[]{:S(2)}) %collective-permute-start.18) | collective-permute-done | bytes 344096 | tf_op jit(solution)/shard_map/ppermute | solution.py:563
  436.6 7.8 %backward_layer.20 = (bf16[48,3584]{1,0:T(8,128)(2,1)S(1)}, bf16[192,3584]{1,0:T(8,128)(2,1)}) custom-call(s32[7]{0:T(128)S(1)} %pad_add_fusion.meta.me, bf16[48,3584]{1,0:T(8,128)(2,1)S(1)} %collective-permute-done.18.inbox, f32[8,3584]{1,0:T(8,128)S(1)} %loss_seed.1.seed, f32[1,3584]{1,0:T(1,128)S(1)} %copy-done.2, ...), custom_call_target="tpu_custom_call", output_to_operand_aliasing={{1}: (9, {})} | custom-call | flops 704643072 | bytes 14680064 | tf_op jit(solution)/shard_map/backward_layer/pallas_call | solution.py:334
  445.7 9.3 %collective-permute-done.19.inbox = bf16[48,3584]{1,0:T(8,128)(2,1)S(1)} collective-permute-done((bf16[48,3584]{1,0:T(8,128)(2,1)S(1)}, bf16[48,3584]{1,0:T(8,128)(2,1)S(1)}, u32[]{:S(2)}, u32[]{:S(2)}) %collective-permute-start.19) | collective-permute-done | bytes 344096 | tf_op jit(solution)/shard_map/ppermute | solution.py:563
  455.0 8.6 %backward_layer.21 = (bf16[48,3584]{1,0:T(8,128)(2,1)}, bf16[192,3584]{1,0:T(8,128)(2,1)}) custom-call(s32[7]{0:T(128)S(1)} %pad_add_fusion.meta.me, bf16[48,3584]{1,0:T(8,128)(2,1)S(1)} %collective-permute-done.19.inbox, f32[8,3584]{1,0:T(8,128)S(1)} %loss_seed.1.seed, f32[1,3584]{1,0:T(1,128)S(1)} %copy-done.2, ...), custom_call_target="tpu_custom_call", output_to_operand_aliasing={{1}: (9, {})} | custom-call | flops 704643072 | bytes 14680064 | tf_op jit(solution)/shard_map/backward_layer/pallas_call | solution.py:334
  (68 shorter events, 33.6 us)
Async XLA Ops:
  6.5 4.3 copy-start
  6.5 79.7 %all-gather.2.cloned.1.call-start = ((), (), s32[]{:S(2)}) async-start(), calls=%async_computation.1 | async-start | bytes 15138816 | tf_op jit(solution)/shard_map/all_gather | solution.py:527
  86.3 5.2 %copy-start.1 = (bf16[3584,2048]{1,0:T(8,128)(2,1)S(1)}, bf16[3584,2048]{1,0:T(8,128)(2,1)}, u32[]{:S(2)}) copy-start(bf16[3584,2048]{1,0:T(8,128)(2,1)} %all-gather.2.cloned.1.call-done.packed) | copy-start | bytes 44040196
  99.5 6.0 %collective-permute-start = (bf16[48,3584]{1,0:T(8,128)(2,1)S(1)}, bf16[48,3584]{1,0:T(8,128)(2,1)S(1)}, u32[]{:S(2)}, u32[]{:S(2)}) collective-permute-start(bf16[48,3584]{1,0:T(8,128)(2,1)S(1)} %get-tuple-element.78), channel_id=1, source_target_pairs={{0,32},{1,33},{2,34},{3,35},{4,36},{5,37},{6,38},{7,39},{8,40},{9,... | collective-permute-start | bytes 1032200 | tf_op jit(solution)/shard_map/ppermute | solution.py:544
  109.9 9.1 %collective-permute-start.1 = (bf16[48,3584]{1,0:T(8,128)(2,1)S(1)}, bf16[48,3584]{1,0:T(8,128)(2,1)S(1)}, u32[]{:S(2)}, u32[]{:S(2)}) collective-permute-start(bf16[48,3584]{1,0:T(8,128)(2,1)S(1)} %get-tuple-element.82), channel_id=1, source_target_pairs={{0,32},{32,64},{1,33},{33,65},{2,34},{34,66},{3,35},{35,67},{4,36}... | collective-permute-start | bytes 1032200 | tf_op jit(solution)/shard_map/ppermute | solution.py:544
  123.3 9.1 %collective-permute-start.2 = (bf16[48,3584]{1,0:T(8,128)(2,1)S(1)}, bf16[48,3584]{1,0:T(8,128)(2,1)S(1)}, u32[]{:S(2)}, u32[]{:S(2)}) collective-permute-start(bf16[48,3584]{1,0:T(8,128)(2,1)S(1)} %get-tuple-element.86), channel_id=1, source_target_pairs={{0,32},{32,64},{64,96},{1,33},{33,65},{65,97},{2,34},{34,66},{66,9... | collective-permute-start | bytes 1032200 | tf_op jit(solution)/shard_map/ppermute | solution.py:544
  136.8 10.2 %collective-permute-start.3 = (bf16[48,3584]{1,0:T(8,128)(2,1)S(1)}, bf16[48,3584]{1,0:T(8,128)(2,1)S(1)}, u32[]{:S(2)}, u32[]{:S(2)}) collective-permute-start(bf16[48,3584]{1,0:T(8,128)(2,1)S(1)} %get-tuple-element.90), channel_id=1, source_target_pairs={{0,32},{32,64},{64,96},{96,128},{1,33},{33,65},{65,97},{97,129},{2... | collective-permute-start | bytes 1032200 | tf_op jit(solution)/shard_map/ppermute | solution.py:544
  147.9 0.7 collective-permute-start.4
  149.2 0.7 collective-permute-start.5
  150.5 0.7 collective-permute-start.6
  151.8 0.7 collective-permute-start.7
  153.1 0.7 collective-permute-start.8
  154.4 0.7 collective-permute-start.9
  155.1 1.5 copy-start.5
  185.2 0.7 collective-permute-start.10
  186.5 0.7 collective-permute-start.11
  187.8 0.7 collective-permute-start.12
  197.4 0.7 collective-permute-start.13
  198.7 0.7 collective-permute-start.14
  200.0 0.7 collective-permute-start.15
  201.3 192.2 %collective-permute-start.16 = (bf16[48,3584]{1,0:T(8,128)(2,1)S(1)}, bf16[48,3584]{1,0:T(8,128)(2,1)S(1)}, u32[]{:S(2)}, u32[]{:S(2)}) collective-permute-start(bf16[48,3584]{1,0:T(8,128)(2,1)S(1)} %get-tuple-element.134), channel_id=1, source_target_pairs={{128,96},{96,64},{64,32},{32,0},{129,97},{97,65},{65,33},{33,1},{1... | collective-permute-start | bytes 1032200 | tf_op jit(solution)/shard_map/ppermute | solution.py:563
  401.3 14.3 %collective-permute-start.17 = (bf16[48,3584]{1,0:T(8,128)(2,1)S(1)}, bf16[48,3584]{1,0:T(8,128)(2,1)S(1)}, u32[]{:S(2)}, u32[]{:S(2)}) collective-permute-start(bf16[48,3584]{1,0:T(8,128)(2,1)S(1)} %get-tuple-element.136), channel_id=1, source_target_pairs={{96,64},{64,32},{32,0},{97,65},{65,33},{33,1},{98,66},{66,34},{34,... | collective-permute-start | bytes 1032200 | tf_op jit(solution)/shard_map/ppermute | solution.py:563
  424.1 12.5 %collective-permute-start.18 = (bf16[48,3584]{1,0:T(8,128)(2,1)S(1)}, bf16[48,3584]{1,0:T(8,128)(2,1)S(1)}, u32[]{:S(2)}, u32[]{:S(2)}) collective-permute-start(bf16[48,3584]{1,0:T(8,128)(2,1)S(1)} %get-tuple-element.138), channel_id=1, source_target_pairs={{64,32},{32,0},{65,33},{33,1},{66,34},{34,2},{67,35},{35,3},{68,36... | collective-permute-start | bytes 1032200 | tf_op jit(solution)/shard_map/ppermute | solution.py:563
  444.4 10.6 %collective-permute-start.19 = (bf16[48,3584]{1,0:T(8,128)(2,1)S(1)}, bf16[48,3584]{1,0:T(8,128)(2,1)S(1)}, u32[]{:S(2)}, u32[]{:S(2)}) collective-permute-start(bf16[48,3584]{1,0:T(8,128)(2,1)S(1)} %get-tuple-element.140), channel_id=1, source_target_pairs={{32,0},{33,1},{34,2},{35,3},{36,4},{37,5},{38,6},{39,7},{40,8},{41... | collective-permute-start | bytes 1032200 | tf_op jit(solution)/shard_map/ppermute | solution.py:563
  (3 other events, 2.6 us)
Sparse Core Ops, SparseCore 0:
  11.0 75.2 all-gather.1
